TPU v7x, 32 devices: a whole 2x2x4 slice. The times are simulated.
32 devices in a mesh: blk: 8 (over z, x), lat: 4 (over y, core).
Axes of the slice: x: 2, y: 2, z: 4, core: 2. Of those that a mesh axis runs over, the one named last changes fastest.
Arguments:
- displacement: float32 [3, 5, 5, 5, 8, 8, 128], P(None, None, None, None, 'blk', 'lat'), may hold values from -6 to 6
- velocity: float32 [3, 5, 5, 5, 8, 8, 128], P(None, None, None, None, 'blk', 'lat'), may hold values from -6 to 6
- rigidity: float32 [5, 5, 5, 8, 8, 128], P(None, None, None, 'blk', 'lat'), may hold values from 0.5 to 2
- density: float32 [5, 5, 5, 8, 8, 128], P(None, None, None, 'blk', 'lat'), may hold values from 0.5 to 2
- history: float32 [256, 63, 3, 128], P(('blk', 'lat')), may hold values from -0.12 to 0.12
- kernel: float32 [64, 3, 3, 128], replicated, may hold values from -0.4375 to 0.4375
- owner_order: int32 [256], replicated, may hold values from 0 to 255, each once
- rigid_offset: float32 [3], replicated, may hold values from -1.8 to 1.8
- rigid_velocity: float32 [3], replicated, may hold values from -6 to 6
Outputs:
- new_displacement: float32 [3, 5, 5, 5, 8, 8, 128], P(None, None, None, None, 'blk', 'lat')
- new_velocity: float32 [3, 5, 5, 5, 8, 8, 128], P(None, None, None, None, 'blk', 'lat')
- new_history: float32 [256, 63, 3, 128], P(('blk', 'lat'))
- new_offset: float32 [3], replicated
- new_rigid_velocity: float32 [3], replicated
Inputs may be any that keep to these rules, and one draw needn't show every extreme that they name: owner_order names every column 0 to 255 once; row j of history belongs to column owner_order[j].
All inputs are finite; a program needn't handle non-finite values.
Results may differ from a plain program's by a relative error of at most 0.0003.
Values sent between devices are 32-bit elements; how exact they have to be, the bound alone decides.
No kernel may reach another device: no remote copies, remote signals or barrier semaphores. Data moves between devices by JAX's collectives and lax.ppermute only.
A program may use at most 64 MiB of HBM per device.

v0:
```python
import math

import jax
import jax.numpy as jnp
import numpy as np
from jax import lax
from jax.sharding import PartitionSpec as P

STEPS = 3


pole_gap = 0.1
time_step = 0.03
rigid_gain = 20.0
coupling = 1.0
highest = lax.Precision.HIGHEST


def with_halo(block, sides, width, periodic):
    for axis, dim in sides:
        count = lax.axis_size(axis)
        forward = [(i, i + 1) for i in range(count - 1)]
        if periodic:
            forward.append((count - 1, 0))
        backward = [(target, source) for source, target in forward]
        low = lax.ppermute(
            lax.slice_in_dim(block, block.shape[dim] - width, None, axis=dim), axis, forward
        )
        high = lax.ppermute(lax.slice_in_dim(block, 0, width, axis=dim), axis, backward)
        block = jnp.concatenate([low, block, high], axis=dim)
    return block


def node_tables():
    points = np.array([-1.0, -math.sqrt(3.0 / 7.0), 0.0, math.sqrt(3.0 / 7.0), 1.0])
    weights = np.array([0.1, 49.0 / 90.0, 32.0 / 45.0, 49.0 / 90.0, 0.1])
    products = np.array(
        [
            np.prod([points[row_at] - points[others] for others in range(5) if others != row_at])
            for row_at in range(5)
        ]
    )
    slopes = np.zeros((5, 5))
    for row_at in range(5):
        for col_at in range(5):
            if row_at == col_at:
                slopes[row_at, col_at] = sum(
                    (
                        1.0 / (points[row_at] - points[others])
                        for others in range(5)
                        if others != row_at
                    )
                )
            else:
                slopes[row_at, col_at] = (
                    products[row_at] / products[col_at] / (points[row_at] - points[col_at])
                )
    return (points, weights, slopes)


def node_volume():
    points, weights, slopes = node_tables()
    node_weight = jnp.asarray(weights, dtype=jnp.float32)
    volume = node_weight[:, None, None] * node_weight[None, :, None] * node_weight[None, None, :]
    return volume[:, :, :, None, None, None]


def stiffness(values, rigidity):
    points, weights, slopes = node_tables()
    deriv = jnp.asarray(slopes, dtype=jnp.float32)
    scaled = (node_volume() * rigidity)[None]
    first_dir = jnp.einsum("ia,kabcxyz->kibcxyz", deriv, values, precision=highest) * scaled
    second_dir = jnp.einsum("jb,kabcxyz->kajcxyz", deriv, values, precision=highest) * scaled
    third_dir = jnp.einsum("lc,kabcxyz->kablxyz", deriv, values, precision=highest) * scaled
    result = jnp.einsum("ia,kibcxyz->kabcxyz", deriv, first_dir, precision=highest)
    result = result + jnp.einsum("jb,kajcxyz->kabcxyz", deriv, second_dir, precision=highest)
    return result + jnp.einsum("lc,kablxyz->kabcxyz", deriv, third_dir, precision=highest)


def join_faces(lower, upper, before_first, after_last, axis):
    count = lower.shape[axis]
    earlier = jnp.concatenate(
        (before_first, lax.slice_in_dim(upper, 0, count - 1, axis=axis)), axis=axis
    )
    later = jnp.concatenate((lax.slice_in_dim(lower, 1, count, axis=axis), after_last), axis=axis)
    return (lower + earlier, upper + later)


def assemble(forces):
    lower, upper = (forces[:, 0], forces[:, 4])
    count = lower.shape[3]
    paired = jnp.concatenate((lower, upper), axis=3)
    widened = with_halo(paired, (("blk", 3),), 1, True)
    lower, upper = join_faces(
        lower,
        upper,
        lax.slice_in_dim(widened, 0, 1, axis=3),
        lax.slice_in_dim(widened, 3, 4, axis=3),
        3,
    )
    forces = forces.at[:, 0].set(lower).at[:, 4].set(upper)
    lower, upper = (forces[:, :, 0], forces[:, :, 4])
    count = lower.shape[4]
    paired = jnp.concatenate(
        (lax.slice_in_dim(lower, 0, 1, axis=4), lax.slice_in_dim(upper, count - 1, count, axis=4)),
        axis=4,
    )
    widened = with_halo(paired, (("lat", 4),), 1, False)
    lower, upper = join_faces(
        lower,
        upper,
        lax.slice_in_dim(widened, 0, 1, axis=4),
        lax.slice_in_dim(widened, 3, 4, axis=4),
        4,
    )
    forces = forces.at[:, :, 0].set(lower).at[:, :, 4].set(upper)
    lower, upper = (forces[:, :, :, 0], forces[:, :, :, 4])
    empty = jnp.zeros_like(lax.slice_in_dim(lower, 0, 1, axis=5))
    lower, upper = join_faces(lower, upper, empty, empty, 5)
    return forces.at[:, :, :, 0].set(lower).at[:, :, :, 4].set(upper)


def interface_grid(row_first, row_count, col_first, col_count, lat_elems, lon_elems):
    points, weights, slopes = node_tables()
    nodes = jnp.asarray(points, dtype=jnp.float32)
    node_weight = jnp.asarray(weights, dtype=jnp.float32)
    theta_step = (math.pi - 2.0 * pole_gap) / lat_elems
    phi_step = 2.0 * math.pi / lon_elems
    row_elem = (row_first + jnp.arange(5 * row_count, dtype=jnp.int32) // 5).astype(jnp.float32)
    col_elem = (col_first + jnp.arange(5 * col_count, dtype=jnp.int32) // 5).astype(jnp.float32)
    colatitude = pole_gap + (row_elem + 0.5 * (1.0 + jnp.tile(nodes, row_count))) * theta_step
    longitude = (col_elem + 0.5 * (1.0 + jnp.tile(nodes, col_count))) * phi_step
    row_weight = jnp.tile(node_weight, row_count)
    col_weight = jnp.tile(node_weight, col_count)
    area_weight = (
        0.25
        * theta_step
        * phi_step
        * (row_weight * jnp.sin(colatitude))[:, None]
        * col_weight[None, :]
    )
    face_weight = row_weight[:, None] * col_weight[None, :]
    return (colatitude, longitude, area_weight, face_weight)


def rotation(colatitude, longitude):
    sin_theta = jnp.sin(colatitude)[:, None]
    cos_theta = jnp.cos(colatitude)[:, None]
    sin_phi = jnp.sin(longitude)[None, :]
    cos_phi = jnp.cos(longitude)[None, :]
    filled = jnp.ones((colatitude.shape[0], longitude.shape[0]), jnp.float32)
    radial = (sin_theta * cos_phi, sin_theta * sin_phi, cos_theta * filled)
    polar_dir = (cos_theta * cos_phi, cos_theta * sin_phi, -sin_theta * filled)
    azimuth = (-sin_phi * filled, cos_phi * filled, 0.0 * filled)
    return jnp.stack(
        [jnp.stack([radial[axis_at], polar_dir[axis_at], azimuth[axis_at]]) for axis_at in range(3)]
    )


def legendre(colatitude, degrees):
    cosine = jnp.cos(colatitude)[:, None]
    sine = jnp.sin(colatitude)[:, None]
    orders = jnp.arange(degrees, dtype=jnp.float32)[None, :]
    factor = jnp.where(
        orders == 0,
        math.sqrt(0.5),
        -jnp.sqrt((2.0 * orders + 1.0) / jnp.maximum(2.0 * orders, 1.0)) * sine,
    )
    diagonal = jnp.cumprod(factor, axis=1)

    def advance(state_pair, degree):
        previous, before = state_pair
        level = degree.astype(jnp.float32)
        upward = jnp.sqrt(
            jnp.maximum(4.0 * level * level - 1.0, 0.0)
            / jnp.maximum(level * level - orders * orders, 1.0)
        )
        lowered = (level - 1.0) * (level - 1.0)
        downward = jnp.sqrt(
            jnp.maximum(lowered - orders * orders, 0.0) / jnp.maximum(4.0 * lowered - 1.0, 1.0)
        )
        recurred = upward * (cosine * previous - downward * before)
        values = jnp.where(
            orders == level,
            diagonal,
            jnp.where(
                orders + 1.0 == level,
                jnp.sqrt(2.0 * orders + 3.0) * cosine * diagonal,
                jnp.where(orders + 1.0 < level, recurred, 0.0),
            ),
        )
        return ((values, previous), values)

    zeroed = jnp.zeros((colatitude.shape[0], degrees), jnp.float32)
    finals, levels = lax.scan(advance, (zeroed, zeroed), jnp.arange(degrees, dtype=jnp.int32))
    return levels


def doubled(colatitude, degrees):
    levels = legendre(colatitude, degrees)
    return jnp.concatenate((levels, levels), axis=2)


def circle_table(longitude, degrees):
    orders = jnp.arange(degrees, dtype=jnp.float32)[None, :]
    angles = longitude[:, None] * orders
    cosines = jnp.where(
        orders == 0, 1.0 / math.sqrt(2.0 * math.pi), jnp.cos(angles) / math.sqrt(math.pi)
    )
    sines = jnp.where(orders == 0, 0.0, jnp.sin(angles) / math.sqrt(math.pi))
    return jnp.concatenate((cosines, sines), axis=1)


def synthesize(coeffs, circle, levels):
    partial_value = jnp.einsum("ckl,ltc->ktc", coeffs, levels, precision=highest)
    return jnp.einsum("ktc,fc->ktf", partial_value, circle, precision=highest)


def respond(owned_rows, history, kernel):
    stacked = jnp.concatenate((owned_rows[:, None], history), axis=1)
    replies = jnp.einsum("jabl,cjbl->cal", kernel, stacked, precision=highest)
    return (replies, stacked[:, :-1])


def to_grid(values):
    bottom = values[:, :, :, 0, :, :, 0]
    lon_count, lat_count = (bottom.shape[3], bottom.shape[4])
    return bottom.transpose(0, 4, 2, 3, 1).reshape(3, 5 * lat_count, 5 * lon_count)


def from_grid(grid, lon_count, lat_count):
    return grid.reshape(3, lat_count, 5, lon_count, 5).transpose(0, 4, 2, 3, 1)


def on_device(
    displacement,
    velocity,
    rigidity,
    density,
    history,
    kernel,
    owner_order,
    rigid_offset,
    rigid_velocity,
):
    lon_count, lat_count = (displacement.shape[4], displacement.shape[5])
    blk_count, lat_devices = (lax.axis_size("blk"), lax.axis_size("lat"))
    lon_elems, lat_elems = (lon_count * blk_count, lat_count * lat_devices)
    degrees = kernel.shape[3]
    colatitude, longitude, area_weight, face_weight = interface_grid(
        lax.axis_index("lat") * lat_count,
        lat_count,
        lax.axis_index("blk") * lon_count,
        lon_count,
        lat_elems,
        lon_elems,
    )
    rotated = rotation(colatitude, longitude)
    levels = doubled(colatitude, degrees)
    circle = circle_table(longitude, degrees)
    inverse = 1.0 / assemble((density * node_volume())[None])
    block_count = 2 * degrees // blk_count
    circle_ordered = jnp.take(circle, owner_order, axis=1)
    block_columns = lax.dynamic_slice_in_dim(
        owner_order, lax.axis_index("blk") * block_count, block_count, 0
    )
    levels_block = jnp.take(levels, block_columns, axis=2)
    for step_index in range(STEPS):
        relative = to_grid(displacement) - jnp.einsum(
            "jktf,j->ktf", rotated, rigid_offset, precision=highest
        )
        weighted = relative * area_weight
        block_sums = lax.psum_scatter(
            jnp.einsum("ktf,fc->ckt", weighted, circle_ordered, precision=highest),
            "blk",
            scatter_dimension=0,
            tiled=True,
        )
        block_partial = jnp.einsum("ckt,ltc->ckl", block_sums, levels_block, precision=highest)
        owned_rows = lax.psum_scatter(block_partial, "lat", scatter_dimension=0, tiled=True)
        replies, history = respond(owned_rows, history, kernel)
        gathered = lax.all_gather(replies, ("blk", "lat"), axis=0, tiled=True)
        coeffs = jnp.zeros_like(gathered).at[owner_order].set(gathered)
        traction = synthesize(coeffs, circle, levels)
        pull_sum = lax.psum(
            jnp.einsum("jktf,ktf->j", rotated * area_weight, traction, precision=highest),
            ("blk", "lat"),
        )
        rigid_velocity = rigid_velocity + time_step * rigid_gain * pull_sum
        rigid_offset = rigid_offset + time_step * rigid_velocity
        forces = -stiffness(displacement, rigidity)
        forces = forces.at[:, :, :, 0, :, :, 0].add(
            from_grid(-coupling * face_weight * traction, lon_count, lat_count)
        )
        velocity = velocity + time_step * assemble(forces) * inverse
        displacement = displacement + time_step * velocity
    return (displacement, velocity, history, rigid_offset, rigid_velocity)


def solution(mesh):
    in_specs = (
        P(None, None, None, None, "blk", "lat", None),
        P(None, None, None, None, "blk", "lat", None),
        P(None, None, None, "blk", "lat", None),
        P(None, None, None, "blk", "lat", None),
        P(("blk", "lat"), None, None, None),
        P(),
        P(),
        P(),
        P(),
    )
    out_specs = (
        P(None, None, None, None, "blk", "lat", None),
        P(None, None, None, None, "blk", "lat", None),
        P(("blk", "lat"), None, None, None),
        P(),
        P(),
    )
    return jax.shard_map(
        on_device, mesh=mesh, in_specs=in_specs, out_specs=out_specs, check_vma=False
    )
```

profile of v0, /device:TPU:1, one launch (start us, length us, event | category | flops | bytes accessed | tf_op | source)
XLA Modules:
  0.0 923.7 jit_solution(4855380724961010719)
XLA Ops:
  8.8 1.8 multiply_bitcast_fusion.2
  11.2 2.0 collective-permute-start.4
  13.3 3.0 collective-permute-start.5
  28.6 275.3 %while.46 = (s32[]{:T(128)}, f32[10,128]{1,0:T(8,128)S(1)}, f32[10,128]{1,0:T(8,128)S(1)}, f32[128,10,128]{2,1,0:T(8,128)}, s32[128]{0:T(128)S(1)}, /*index=5*/f...) while((s32[]{:T(128)}, f32[10,128]{1,0:T(8,128)S(1)}, ...), condition=%wide.region_2.3_spmd.clone.clone, body=%wide.region_1.2_spmd.clone.clone.sunk | while | flops 14736 | bytes 38715 | solution.py:195
  303.9 1.8 copy.724
  309.9 1.8 fusion.42
  312.8 1.7 copy.734
  314.6 2.7 gather_fusion.1
  322.1 4.2 collective-permute-start.6
  327.3 1.9 collective-permute-start.7
  329.2 3.0 collective-permute-done.7
  335.6 1.9 fusion.105
  337.5 12.0 %all-reduce.8 = f32[32,3,128]{2,1,0:T(4,128)} all-reduce(f32[32,3,128]{2,1,0:T(4,128)} %fusion.105), channel_id=3, replica_groups=mesh['blk'=8,'lat'=4] {'lat'}, use_global_device_ids=true, to_apply=%region_4.5.clone | all-reduce | flops 12288 | bytes 98304
  350.2 1.7 copy.733
  351.9 6.5 fusion.59
  359.5 40.5 %all_gather.9 = f32[256,3,128]{2,0,1:T(8,128)S(1)} all-gather(f32[8,3,128]{2,0,1:T(8,128)S(1)} %copy.736), channel_id=1, replica_groups=mesh['blk'=8,'lat'=4] {'blk','lat'}, dimensions={0}, use_global_device_ids=true | all-gather | bytes 405504 | tf_op jit(solution)/shard_map/all_gather | solution.py:282
  400.3 7.0 scatter_fusion
  407.3 3.4 convolution_bitcast_fusion.8
  414.1 1.6 slice_add_fusion.2
  415.7 1.6 scatter-add.10
  417.4 2.1 fusion.195
  421.9 36.1 %psum.21 = f32[3]{0:T(128)S(1)} all-reduce(f32[3]{0:T(128)S(1)} %convolution_bitcast_fusion.11), channel_id=1, replica_groups=mesh['blk'=8,'lat'=4] {'blk','lat'}, use_global_device_ids=true, to_apply=%region_6.7 | all-reduce | flops 3 | bytes 24 | tf_op jit(solution)/shard_map/psum | solution.py:285
  459.9 3.3 scatter.101
  464.8 3.3 scatter.104
  469.1 5.4 collective-permute-start.2
  474.5 3.1 slice_maximum_fusion.2
  477.8 2.3 collective-permute-start.3
  480.1 3.2 collective-permute-done.3
  496.4 53.3 %reduce-scatter.12.cloned.1.call-done = f32[32,30]{1,0:T(8,128)} async-done(((f32[256,30]{1,0:T(8,128)}), f32[32,30]{1,0:T(8,128)}) %reduce-scatter.12.cloned.1.call-update) | async-done | bytes 3856
  550.9 13.0 %all-reduce.9 = f32[32,3,128]{2,1,0:T(4,128)S(1)} all-reduce(f32[32,3,128]{2,1,0:T(4,128)S(1)} %fusion.103), channel_id=5, replica_groups=mesh['blk'=8,'lat'=4] {'lat'}, use_global_device_ids=true, to_apply=%region_8.9.clone | all-reduce | flops 12288 | bytes 98304
  565.8 7.1 fusion.56
  572.9 1.6 copy.788
  574.5 41.5 %all_gather.10 = f32[256,3,128]{2,0,1:T(8,128)S(1)} all-gather(f32[8,3,128]{2,0,1:T(8,128)} %copy.788), channel_id=1, replica_groups=mesh['blk'=8,'lat'=4] {'blk','lat'}, dimensions={0}, use_global_device_ids=true | all-gather | bytes 405504 | tf_op jit(solution)/shard_map/all_gather | solution.py:282
  616.3 7.0 scatter_fusion.1
  623.4 3.4 convolution_bitcast_fusion.7
  628.5 1.8 fusion.47
  630.2 35.9 %psum.22 = f32[3]{0:T(128)} all-reduce(f32[3]{0:T(128)} %convolution_bitcast_fusion.10), channel_id=1, replica_groups=mesh['blk'=8,'lat'=4] {'blk','lat'}, use_global_device_ids=true, to_apply=%region_10.11 | all-reduce | flops 3 | bytes 24 | tf_op jit(solution)/shard_map/psum | solution.py:285
  670.1 1.6 slice_add_fusion.1
  671.7 1.6 scatter-add.11
  674.9 2.8 collective-permute-start.9
  677.7 3.0 slice_maximum_fusion.1
  680.9 2.7 collective-permute-done.8
  683.8 3.2 scatter.124
  687.0 3.2 scatter.125
  691.2 5.9 collective-permute-start.10
  697.1 2.1 collective-permute-start.11
  711.7 1.6 fusion.74
  714.8 50.8 %reduce-scatter.14.cloned.1.call-done = f32[32,30]{1,0:T(8,128)} async-done(((f32[256,30]{1,0:T(8,128)}), f32[32,30]{1,0:T(8,128)}) %reduce-scatter.14.cloned.1.call-update) | async-done | bytes 3856
  766.8 12.9 %all-reduce.10 = f32[32,3,128]{2,1,0:T(4,128)S(1)} all-reduce(f32[32,3,128]{2,1,0:T(4,128)S(1)} %fusion.101), channel_id=7, replica_groups=mesh['blk'=8,'lat'=4] {'lat'}, use_global_device_ids=true, to_apply=%region_12.13.clone | all-reduce | flops 12288 | bytes 98304
  779.8 1.7 copy.820
  781.5 6.1 fusion.53
  787.7 41.3 %all_gather.11 = f32[256,3,128]{2,0,1:T(8,128)S(1)} all-gather(f32[8,3,128]{2,0,1:T(8,128)S(1)} %copy.822), channel_id=1, replica_groups=mesh['blk'=8,'lat'=4] {'blk','lat'}, dimensions={0}, use_global_device_ids=true | all-gather | bytes 405504 | tf_op jit(solution)/shard_map/all_gather | solution.py:282
  829.4 7.0 scatter_fusion.2
  836.4 3.4 convolution_bitcast_fusion.6
  841.3 35.5 %psum.23 = f32[3]{0:T(128)S(1)} all-reduce(f32[3]{0:T(128)S(1)} %convolution_bitcast_fusion.9), channel_id=1, replica_groups=mesh['blk'=8,'lat'=4] {'blk','lat'}, use_global_device_ids=true, to_apply=%region_14.15 | all-reduce | flops 3 | bytes 24 | tf_op jit(solution)/shard_map/psum | solution.py:285
  878.3 2.7 collective-permute-start.13
  881.1 3.5 slice_maximum_fusion
  884.6 2.8 copy.838
  887.6 5.8 collective-permute-done.12
  893.5 4.0 scatter.162
  897.5 4.0 scatter.163
  901.5 5.9 collective-permute-start.14
  907.5 1.9 collective-permute-start.15
  909.5 3.5 collective-permute-done.15
  (1474 shorter events, 274.4 us)
Async XLA Ops:
  7.2 19.1 %copy-start.28 = (f32[5,5,1,1,1,1]{1,0,5,4,3,2:T(8,128)S(1)}, f32[5,5,1,1,1,1]{1,0,5,4,3,2:T(8,128)}, u32[]{:S(2)}) copy-start(f32[5,5,1,1,1,1]{1,0,5,4,3,2:T(8,128)} %constant.792) | copy-start | bytes 304
  7.2 19.1 %copy-start.4 = (f32[3,5,5,5,1,2,128]{6,5,4,3,2,1,0:T(2,128)S(1)}, f32[3,5,5,5,1,2,128]{6,5,4,3,2,1,0:T(2,128)}, u32[]{:S(2)}) copy-start(f32[3,5,5,5,1,2,128]{6,5,4,3,2,1,0:T(2,128)} %param.74) | copy-start | bytes 1152004
  7.2 327.0 %reduce-scatter.10.cloned.1.call-start = ((), (), s32[]{:S(2)}) async-start(), calls=%async_computation.3 | async-start | bytes 147456
  10.6 16.9 %copy-start.29 = (f32[1,5,5,5,1,2,128]{6,5,3,2,4,1,0:T(2,128)}, f32[1,5,5,5,1,2,128]{6,5,3,2,4,1,0:T(2,128)S(1)}, u32[]{:S(2)}) copy-start(f32[1,5,5,5,1,2,128]{6,5,3,2,4,1,0:T(2,128)S(1)} %get-tuple-element.633) | copy-start | bytes 384004
  11.2 307.3 %collective-permute-start.4 = (f32[1,5,5,1,2,128]{5,4,2,1,3,0:T(2,128)}, f32[1,5,5,1,2,128]{5,4,2,1,3,0:T(2,128)}, u32[]{:S(2)}, u32[]{:S(2)}) collective-permute-start(f32[1,5,5,1,2,128]{5,4,2,1,3,0:T(2,128)} %get-tuple-element.641), channel_id=1, source_target_pairs={{0,4},{4,8},{8,12},{12,16},{16,20},{20,24},{24,28},{28,0},{1,5},{5... | collective-permute-start | bytes 76808 | tf_op jit(solution)/shard_map/ppermute | solution.py:26
  13.3 306.7 %collective-permute-start.5 = (f32[1,5,5,1,2,128]{5,4,2,1,3,0:T(2,128)}, f32[1,5,5,1,2,128]{5,4,2,1,3,0:T(2,128)}, u32[]{:S(2)}, u32[]{:S(2)}) collective-permute-start(f32[1,5,5,1,2,128]{5,4,2,1,3,0:T(2,128)} %get-tuple-element.640), channel_id=1, source_target_pairs={{4,0},{8,4},{12,8},{16,12},{20,16},{24,20},{28,24},{0,28},{5,1},{9... | collective-permute-start | bytes 76808 | tf_op jit(solution)/shard_map/ppermute | solution.py:29
  17.7 9.9 %copy-start.41 = (pred[256]{0:T(512)(128)(4,1)}, pred[256]{0:T(512)(128)(4,1)S(1)}, u32[]{:S(2)}) copy-start(pred[256]{0:T(512)(128)(4,1)S(1)} %compare_and_fusion.1) | copy-start | bytes 772
  24.2 3.3 copy-start.46
  24.3 4.3 copy-start.50
  25.0 3.6 copy-start.26
  26.2 523.5 %reduce-scatter.12.cloned.1.call-start = ((), (), s32[]{:S(2)}) async-start(), calls=%async_computation.4 | async-start | bytes 147456
  307.3 187.6 %copy-start.6 = (f32[5,5,5,2,128]{4,0,3,2,1:T(8,128)}, f32[5,5,5,2,128]{4,0,3,2,1:T(8,128)S(1)}, u32[]{:S(2)}) copy-start(f32[5,5,5,2,128]{4,0,3,2,1:T(8,128)S(1)} %copy.712) | copy-start | bytes 384004
  309.1 2.6 copy-start.30
  314.5 37.4 %copy-start = (f32[8,63,3,128]{1,0,2,3:T(8,128)}, f32[8,63,3,128]{1,0,2,3:T(8,128)S(1)}, u32[]{:S(2)}) copy-start(f32[8,63,3,128]{1,0,2,3:T(8,128)S(1)} %copy.734) | copy-start | bytes 2322436
  314.6 2.8 copy-start.51
  314.6 21.0 %copy-start.36 = (pred[32]{0:T(512)(128)(4,1)S(1)}, pred[32]{0:T(512)(128)(4,1)}, u32[]{:S(2)}) copy-start(pred[32]{0:T(512)(128)(4,1)} %get-tuple-element.597) | copy-start | bytes 100
  322.1 7.0 collective-permute-start.6
  327.3 5.0 collective-permute-start.7
  407.3 50.7 %copy-start.47 = (f32[3]{0:T(128)S(1)}, f32[3]{0:T(128)}, u32[]{:S(2)}) copy-start(f32[3]{0:T(128)} %param.81) | copy-start | bytes 40
  407.3 50.7 %copy-start.48 = (f32[3]{0:T(128)S(1)}, f32[3]{0:T(128)}, u32[]{:S(2)}) copy-start(f32[3]{0:T(128)} %param.82) | copy-start | bytes 40
  411.6 62.9 %copy-start.1 = (f32[8,63,3,128]{1,0,2,3:T(8,128)S(1)}, f32[8,63,3,128]{1,0,2,3:T(8,128)}, u32[]{:S(2)}) copy-start(f32[8,63,3,128]{1,0,2,3:T(8,128)} %copy-done) | copy-start | bytes 2322436
  419.5 43.7 %collective-permute-start.1 = (f32[3,5,5,1,2,128]{5,4,2,1,0,3:T(2,128)}, f32[3,5,5,1,2,128]{5,4,2,1,0,3:T(2,128)}, u32[]{:S(2)}, u32[]{:S(2)}) collective-permute-start(f32[3,5,5,1,2,128]{5,4,2,1,0,3:T(2,128)} %bitcast.44), channel_id=1, source_target_pairs={{4,0},{8,4},{12,8},{16,12},{20,16},{24,20},{28,24},{0,28},{5,1},{9... | collective-permute-start | bytes 230408 | tf_op jit(solution)/shard_map/ppermute | solution.py:29
  420.4 37.8 %collective-permute-start = (f32[3,5,5,1,2,128]{5,4,2,1,0,3:T(2,128)}, f32[3,5,5,1,2,128]{5,4,2,1,0,3:T(2,128)}, u32[]{:S(2)}, u32[]{:S(2)}) collective-permute-start(f32[3,5,5,1,2,128]{5,4,2,1,0,3:T(2,128)} %bitcast.45), channel_id=1, source_target_pairs={{0,4},{4,8},{8,12},{12,16},{16,20},{20,24},{24,28},{28,0},{1,5},{5... | collective-permute-start | bytes 230408 | tf_op jit(solution)/shard_map/ppermute | solution.py:26
  458.0 19.6 %copy-start.49 = (f32[3]{0:T(128)}, f32[3]{0:T(128)S(1)}, u32[]{:S(2)}) copy-start(f32[3]{0:T(128)S(1)} %psum.21) | copy-start | bytes 40
  458.1 19.6 %copy-start.39 = (f32[3]{0:T(128)}, f32[3]{0:T(128)S(1)}, u32[]{:S(2)}) copy-start(f32[3]{0:T(128)S(1)} %multiply_add_fusion.8) | copy-start | bytes 40
  469.1 8.5 copy-start.11
  469.1 8.6 collective-permute-start.2
  477.8 5.5 collective-permute-start.3
  480.1 3.5 copy-start.14
  480.1 3.5 copy-start.17
  483.6 1.7 copy-start.8
  483.9 4.3 copy-start.42
  490.2 275.3 %reduce-scatter.14.cloned.1.call-start = ((), (), s32[]{:S(2)}) async-start(), calls=%async_computation.5 | async-start | bytes 147456
  493.3 57.2 %copy-start.37 = (pred[32]{0:T(512)(128)(4,1)S(1)}, pred[32]{0:T(512)(128)(4,1)}, u32[]{:S(2)}) copy-start(pred[32]{0:T(512)(128)(4,1)} %get-tuple-element.597) | copy-start | bytes 100
  565.7 7.1 copy-start.2
  623.3 4.4 copy-start.32
  623.3 5.1 copy-start.23
  623.3 5.1 copy-start.24
  623.4 5.1 copy-start.25
  623.4 5.1 copy-start.34
  628.5 49.3 %copy-start.3 = (f32[8,1,3,128]{1,0,2,3:T(8,128)S(1)}, f32[8,1,3,128]{1,0,2,3:T(8,128)}, u32[]{:S(2)}) copy-start(f32[8,1,3,128]{1,0,2,3:T(8,128)} %copy-done.2) | copy-start | bytes 36868
  666.8 1.4 copy-start.44
  674.9 5.9 collective-permute-start.9
  677.7 6.0 collective-permute-start.8
  691.2 8.1 collective-permute-start.10
  697.1 5.5 collective-permute-start.11
  704.2 3.3 copy-start.31
  704.2 3.3 copy-start.27
  704.2 3.3 copy-start.43
  704.8 3.9 copy-start.7
  711.7 54.7 %copy-start.38 = (pred[32]{0:T(512)(128)(4,1)S(1)}, pred[32]{0:T(512)(128)(4,1)}, u32[]{:S(2)}) copy-start(pred[32]{0:T(512)(128)(4,1)} %get-tuple-element.597) | copy-start | bytes 100
  713.3 68.2 %copy-start.5 = (f32[64,3,3,128]{0,1,2,3:T(4,128)S(1)}, f32[64,3,3,128]{0,1,2,3:T(4,128)}, u32[]{:S(2)}) copy-start(f32[64,3,3,128]{0,1,2,3:T(4,128)} %copy.735) | copy-start | bytes 884740
  836.3 3.7 copy-start.33
  836.3 4.0 copy-start.20
  836.3 4.0 copy-start.21
  836.4 4.0 copy-start.22
  836.4 4.0 copy-start.35
  839.7 37.1 %copy-start.40 = (f32[3]{0:T(128)S(1)}, f32[3]{0:T(128)}, u32[]{:S(2)}) copy-start(f32[3]{0:T(128)} %copy-done.39) | copy-start | bytes 40
  839.7 37.1 %copy-start.45 = (f32[3]{0:T(128)S(1)}, f32[3]{0:T(128)}, u32[]{:S(2)}) copy-start(f32[3]{0:T(128)} %copy-done.44) | copy-start | bytes 40
  878.3 9.2 collective-permute-start.13
  887.4 6.0 collective-permute-start.12
  901.5 7.9 collective-permute-start.14
  907.5 5.5 collective-permute-start.15
  913.1 1.4 copy-start.19
  (7 other events, 7.9 us)
Sparse Core Ops, SparseCore 0:
  26.3 59.0 reduce-scatter.9
  490.4 59.2 reduce-scatter.11
  708.8 56.6 reduce-scatter.13
where the time goes:
time: 934 us; the launch traced here: 924 us
  blocking collectives  269 us (29%)
  local copies, waits for them, and re-layouts  184 us (20%)
  other arithmetic  138 us (15%)
  waiting for transfers between devices  123 us (13%)
  loops' own time  88.9 us (10%)
  matrix products  63.1 us (7%)
  starting transfers between devices  42 us (4%)
  between operations  16.3 us (2%)
    all_gather x3, blocking collectives, on_device(): gathered = lax.all_gather(replies, ('blk', 'lat'), axis=0, tiled=True)  123 us
    psum x3, blocking collectives, on_device(): lax.psum(jnp.einsum('jktf,ktf->j', rotated * area_weight, traction, preci...  108 us
    unnamed x6, waiting for transfers between devices  104 us
    another operation x1, loops' own time, legendre(): lax.scan(advance, (zeroed, zeroed), jnp.arange(degrees, dtype=jnp.int32))  88.9 us
    dynamic_update_slice x128, other arithmetic, legendre(): lax.scan(advance, (zeroed, zeroed), jnp.arange(degrees, dtype=jnp.int32))  86.7 us
    dynamic_slice x128, local copies, waits for them, and re-layouts, legendre(): lax.scan(advance, (zeroed, zeroed), jnp.arange(degrees, dtype=jnp.int32))  74.5 us
    unnamed x3, blocking collectives  37.9 us
    ppermute x8, starting transfers between devices, with_halo(): lax.ppermute(lax.slice_in_dim(block, block.shape[dim] - width, None, axis...  25 us
  transfers between devices with their start and end apart: 19, of which 8 were waited for; matrix products, arithmetic and copies ran while one was open for 27% of the time, Pallas kernels for 0%

commit v1 on v0

v1 whole, which is shorter than its diff:
```python
import functools
import math

import jax
import jax.numpy as jnp
import numpy as np
from jax import lax
from jax.experimental import pallas as pl
from jax.experimental.pallas import tpu as pltpu
from jax.sharding import PartitionSpec as P

STEPS = 3
pole_gap = 0.1
time_step = 0.03
rigid_gain = 20.0
highest = lax.Precision.HIGHEST
f32 = jnp.float32
ROWS = 8
N3 = 125
CHUNKS = 8
HEAD = 32
PAY = HEAD + 4 * CHUNKS


def node_tables():
    points = np.array([-1.0, -math.sqrt(3.0 / 7.0), 0.0, math.sqrt(3.0 / 7.0), 1.0])
    weights = np.array([0.1, 49.0 / 90.0, 32.0 / 45.0, 49.0 / 90.0, 0.1])
    products = np.array(
        [np.prod([points[i] - points[j] for j in range(5) if j != i]) for i in range(5)]
    )
    slopes = np.zeros((5, 5))
    for i in range(5):
        for j in range(5):
            if i == j:
                slopes[i, j] = sum(1.0 / (points[i] - points[n]) for n in range(5) if n != i)
            else:
                slopes[i, j] = products[i] / products[j] / (points[i] - points[j])
    return points, weights, slopes


POINTS, WEIGHTS, SLOPES = node_tables()
VOLUME = [
    float(WEIGHTS[a] * WEIGHTS[b] * WEIGHTS[c])
    for a in range(5)
    for b in range(5)
    for c in range(5)
]


def centro_apply(matrix, x):
    s0, s1, d0, d1 = x[0] + x[4], x[1] + x[3], x[0] - x[4], x[1] - x[3]
    even, odd = [], []
    for i in range(2):
        even.append(
            (0.5 * float(matrix[i][0] + matrix[i][4])) * s0
            + (0.5 * float(matrix[i][1] + matrix[i][3])) * s1
            + float(matrix[i][2]) * x[2]
        )
    for i in range(3):
        odd.append(
            (0.5 * float(matrix[i][0] - matrix[i][4])) * d0
            + (0.5 * float(matrix[i][1] - matrix[i][3])) * d1
        )
    return [odd[0] + even[0], odd[1] + even[1], odd[2], odd[1] - even[1], odd[0] - even[0]]


def row_ids(shape):
    return lax.broadcasted_iota(jnp.int32, shape, len(shape) - 2)


def lane_ids(shape):
    return lax.broadcasted_iota(jnp.int32, shape, len(shape) - 1)


def stiffness(u, scaled, out, aux, ny):
    lanes = u.shape[-1]
    rows = row_ids((ROWS, lanes))
    for node in range(N3):
        x = u[node]
        spread = jnp.where(
            rows < ny,
            pltpu.roll(x, ny, 0),
            jnp.where(rows < 2 * ny, pltpu.roll(x, 2 * ny, 0), pltpu.roll(x, 3 * ny, 0)),
        )
        scaled[node] = spread * (-VOLUME[node])
    for direction in range(3):
        stride = (25, 5, 1)[direction]

        def line(i, carry, direction=direction, stride=stride):
            if direction == 0:
                base = i
            elif direction == 1:
                base = (i // 5) * 25 + i % 5
            else:
                base = i * 5
            slope = centro_apply(SLOPES, [u[base + j * stride] for j in range(5)])
            flux = [slope[j] * scaled[base + j * stride] for j in range(5)]
            force = centro_apply(SLOPES.T, flux)
            for j in range(5):
                at = base + j * stride
                if direction == 0:
                    out[at] = force[j]
                else:
                    out[at] = out[at] + force[j]
            return carry

        lax.fori_loop(0, 25, line, 0, unroll=5)
    if aux is not None:
        for node in range(N3):
            out[node] = jnp.where(rows < 3 * ny, out[node], aux[node] * VOLUME[node])


def join_rows(out, ny):
    lanes = out.shape[-1]
    y = row_ids((ROWS, lanes)) % ny
    for a in range(5):
        for c in range(5):
            low, high = a * 25 + c, a * 25 + 20 + c
            first, last = out[low], out[high]
            out[high] = last + jnp.where(y < ny - 1, pltpu.roll(first, ROWS - 1, 0), 0.0)
            out[low] = first + jnp.where(y > 0, pltpu.roll(last, 1, 0), 0.0)


def join_radius(out):
    lanes = out.shape[-1]
    z = lane_ids((ROWS, lanes))
    for ab in range(25):
        low, high = ab * 5, ab * 5 + 4
        first, last = out[low], out[high]
        out[high] = last + jnp.where(z < lanes - 1, pltpu.roll(first, lanes - 1, 1), 0.0)
        out[low] = first + jnp.where(z > 0, pltpu.roll(last, 1, 1), 0.0)


def spread_inverse(x, ny):
    rows = row_ids(x.shape)
    inverse = 1.0 / jnp.where(rows < 3 * ny, 1.0, x)
    return jnp.where(
        rows < ny,
        pltpu.roll(inverse, ny, 0),
        jnp.where(rows < 2 * ny, pltpu.roll(inverse, 2 * ny, 0), pltpu.roll(inverse, 3 * ny, 0)),
    )


def pack(source, aux, out, ny):
    for node in range(N3):
        for k in range(3):
            out[node, k * ny : (k + 1) * ny, :] = source[k, node]
        out[node, 3 * ny : 4 * ny, :] = aux[node]


def gather_kernel(
    dims, u, v, rig, dens, hist, kern, up, down, diag, cosrow, owner, out, pu, pv, wide
):
    ny, nlat, nown, rows_all, degrees = dims
    depth = u.shape[-1]
    out[...] = jnp.zeros(out.shape, f32)
    pack(u, rig, pu, ny)
    pack(v, dens, pv, ny)
    pick = jnp.where(
        row_ids((ROWS, depth)) == lane_ids((ROWS, depth)), 1.0, 0.0
    ) * jnp.where(row_ids((ROWS, depth)) < 2, 1.0, 0.0)
    for part, ref in enumerate((pu, pv)):
        flat = ref[...].reshape(N3 * ROWS, depth)
        picked = lax.dot_general(
            pick, flat, (((1,), (1,)), ((), ())), precision=highest, preferred_element_type=f32
        )
        for q in range(CHUNKS):
            width = min(128, N3 * ROWS - q * 128)
            at = HEAD + (part * CHUNKS + q) * 2
            out[at : at + 2, 0:width] = picked[0:2, q * 128 : q * 128 + width]
    lags = kern.shape[0]
    zero = jnp.zeros((3, degrees), f32)
    replies = []
    for first in range(0, nown, 4):
        js = list(range(first, min(nown, first + 4)))

        def lag_body(q, accs, js=js):
            ks = [[kern[q + n + 1, k] for k in range(3)] for n in range(3)]
            res = []
            for jj, j in enumerate(js):
                h = hist[j, q]
                for n in range(3):
                    for k in range(3):
                        res.append(accs[(jj * 3 + n) * 3 + k] + ks[n][k] * h)
            return tuple(res)

        accs = lax.fori_loop(0, lags - 3, lag_body, (zero,) * (9 * len(js)))
        accs = list(accs)
        for q in (lags - 3, lags - 2):
            for jj, j in enumerate(js):
                h = hist[j, q]
                for n in range(3):
                    if q + n + 1 < lags:
                        for k in range(3):
                            at = (jj * 3 + n) * 3 + k
                            accs[at] = accs[at] + kern[q + n + 1, k] * h
        for jj, j in enumerate(js):
            replies.append(
                [jnp.sum(accs[jj * 9 + i], axis=0, keepdims=True) for i in range(9)]
            )
    pad = [jnp.zeros((1, degrees), f32)] * (ROWS - nown)
    held = [jnp.concatenate([replies[j][i] for j in range(nown)] + pad, axis=0) for i in range(9)]
    device = lax.axis_index("blk") * nlat + lax.axis_index("lat")
    width = rows_all
    across = max(degrees, width)
    rows = row_ids((ROWS, across))
    order = jnp.zeros((ROWS, across), jnp.int32)
    for j in range(nown):
        order = jnp.where(rows == j, lax.rem(owner[device * nown + j], degrees), order)
    hot = jnp.where(order[:, 0:degrees] == lane_ids((ROWS, degrees)), 1.0, 0.0)
    contract = (((1,), (1,)), ((), ()))
    up_own = lax.dot_general(hot, up[...], contract, precision=highest, preferred_element_type=f32)
    down_own = lax.dot_general(
        hot, down[...], contract, precision=highest, preferred_element_type=f32
    )
    start = lax.dot_general(hot, diag[...], contract, precision=highest, preferred_element_type=f32)
    cosine = jnp.broadcast_to(cosrow[0:1, :], (ROWS, width))
    comp = (lane_ids((ROWS, width)) % ROWS) // ny
    which = order[:, 0:width]
    prev = jnp.zeros((ROWS, width), f32)
    before = jnp.zeros((ROWS, width), f32)
    sums = [jnp.zeros((ROWS, width), f32) for _ in range(3)]
    for level in range(degrees):
        value = up_own[:, level : level + 1] * (
            cosine * prev - down_own[:, level : level + 1] * before
        )
        value = jnp.where(which == level, start, value)
        for n in range(3):
            h = jnp.where(
                comp == 0,
                held[n * 3][:, level : level + 1],
                jnp.where(
                    comp == 1,
                    held[n * 3 + 1][:, level : level + 1],
                    held[n * 3 + 2][:, level : level + 1],
                ),
            )
            sums[n] = sums[n] + h * value
        before, prev = prev, value
    wide[...] = jnp.zeros(wide.shape, f32)
    for n in range(3):
        wide[:, n * width : (n + 1) * width] = sums[n]
    for q in range(HEAD // ROWS):
        out[q * ROWS : (q + 1) * ROWS, :] = wide[:, q * 128 : (q + 1) * 128]


def write_faces(force, left, right, low, high):
    for b in range(5):
        for c in range(5):
            left[b * 5 + c] = force[b * 5 + c]
            right[b * 5 + c] = force[100 + b * 5 + c]
    for a in range(5):
        for c in range(5):
            low[a * 5 + c] = force[a * 25 + c]
            high[a * 5 + c] = force[a * 25 + 20 + c]


def start_kernel(ny, u, v, rig, dens, pu, pv, force, left, right, low, high, scaled):
    pack(u, rig, pu, ny)
    pack(v, dens, pv, ny)
    stiffness(pu, scaled, force, pv, ny)
    join_rows(force, ny)
    join_radius(force)
    write_faces(force, left, right, low, high)


def advance_kernel(dims, first, last, *refs):
    ny, nlat, lanes = dims
    refs = list(refs)
    force, from_left, from_right, from_low, from_high, traction, pu, pv = refs[:8]
    refs = refs[8:]
    if not first:
        inverse = refs.pop(0)
    if last:
        out_u, out_v, total = refs
    else:
        new_u, new_v, new_force, left, right, low, high = refs[:7]
        refs = refs[7:]
        if first:
            inverse = refs.pop(0)
        total, scaled = refs
    lat = lax.axis_index("lat")
    rows = row_ids((ROWS, lanes))
    y = rows % ny
    z = lane_ids((ROWS, lanes))
    for node in range(N3):
        total[node] = force[node]
    for bc in range(25):
        total[bc] = total[bc] + from_left[bc]
        total[100 + bc] = total[100 + bc] + from_right[bc]
    has_low = jnp.where(lat > 0, 1, 0)
    has_high = jnp.where(lat < nlat - 1, 1, 0)
    take_low = jnp.logical_and(y == 0, jnp.full(y.shape, has_low, jnp.int32) > 0)
    take_high = jnp.logical_and(y == ny - 1, jnp.full(y.shape, has_high, jnp.int32) > 0)
    for a in range(5):
        for c in range(5):
            at = a * 25 + c
            total[at] = total[at] + jnp.where(
                take_low, pltpu.roll(from_low[a * 5 + c], ROWS - (ny - 1), 0), 0.0
            )
            total[at + 20] = total[at + 20] + jnp.where(
                take_high, pltpu.roll(from_high[a * 5 + c], ny - 1, 0), 0.0
            )
    if first:
        for node in range(N3):
            inverse[node] = spread_inverse(total[node], ny)
    for a in range(5):
        wa = float(WEIGHTS[a] * (2.0 if a in (0, 4) else 1.0))
        for b in range(5):
            tr = traction[b * ROWS : (b + 1) * ROWS, :]
            if tr.shape[1] != lanes:
                tr = tr[:, 0:lanes]
            moved = pltpu.roll(tr, lanes - a, 1) if a else tr
            at = a * 25 + b * 5
            total[at] = total[at] - (wa * pick_face(b, rows, ny, has_low, has_high)) * jnp.where(
                z == 0, moved, 0.0
            )
    for node in range(N3):
        speed = pv[node] + time_step * total[node] * inverse[node]
        place = pu[node] + time_step * speed
        if last:
            for k in range(3):
                out_v[k, node] = speed[k * ny : (k + 1) * ny, :]
                out_u[k, node] = place[k * ny : (k + 1) * ny, :]
        else:
            new_v[node] = speed
            new_u[node] = jnp.where(rows < 3 * ny, place, pu[node])
    if not last:
        stiffness(new_u, scaled, new_force, None, ny)
        join_rows(new_force, ny)
        join_radius(new_force)
        write_faces(new_force, left, right, low, high)


def pick_face(b, rows, ny, has_low, has_high):
    weight = float(WEIGHTS[b])
    y = rows % ny
    if b == 0:
        shared = jnp.logical_or(y > 0, jnp.full(y.shape, has_low, jnp.int32) > 0)
    elif b == 4:
        shared = jnp.logical_or(y < ny - 1, jnp.full(y.shape, has_high, jnp.int32) > 0)
    else:
        return weight
    return jnp.where(shared, 2.0 * weight, weight)


def unpack(pieces, part, rows_ref, out, dims):
    ny, nlat, nblk, lanes = dims
    count = nblk * nlat
    rows_ref[...] = jnp.zeros(rows_ref.shape, f32)
    for q in range(CHUNKS):
        for ez in range(2):
            at = ez * count
            for ref in pieces:
                n = ref.shape[0] // PAY
                rows_ref[q, at : at + n, :] = ref[
                    pl.ds(HEAD + (part * CHUNKS + q) * 2 + ez, n, stride=PAY), :
                ]
                at += n
    for q in range(CHUNKS):
        nodes = min(16, N3 - q * 16)
        for strip in range(lanes // 128):
            block = rows_ref[q, strip * 128 : (strip + 1) * 128, :].T
            out[q * 16 : q * 16 + nodes, :, strip * 128 : (strip + 1) * 128] = block[
                : nodes * ROWS
            ].reshape(nodes, ROWS, 128)


def split3(x):
    hi = x.astype(jnp.bfloat16)
    rest = x - hi.astype(f32)
    mid = rest.astype(jnp.bfloat16)
    low = (rest - mid.astype(f32)).astype(jnp.bfloat16)
    return hi, mid, low


def place_matrix(a, dims, fs):
    ny, nlat, nblk, lanes = dims
    shape = (lanes, nlat * fs)
    lam = row_ids(shape)
    col = lane_ids(shape)
    target = lax.rem(lam, nlat) * fs + lax.div(lam, nlat) * 5 + a
    hit = jnp.logical_and(col == target, lam < nlat * nblk)
    return jnp.where(hit, 1.0, 0.0).astype(jnp.bfloat16)


def lat_of(i, nlat):
    return lax.rem(lax.axis_index("lat") + i, nlat)


def to_traction(dims, n, u, tables, state, xv, hist, coef_refs, coef_out, hat, shat, xv_out, out):
    ny, nlat, nblk, lanes = dims
    legendre, circle, rowc, lanec, kern = tables
    degrees = legendre.shape[-1]
    fs = circle.shape[0]
    grid = jnp.zeros((5 * ROWS, nlat * fs), f32)
    for a in range(5):
        rows = jnp.concatenate([u[a * 25 + b * 5] for b in range(5)], axis=0)
        place = place_matrix(a, dims, fs)
        for piece in split3(rows):
            grid = grid + jnp.dot(piece, place, preferred_element_type=f32)
    cosphi, sinphi, wphi = lanec[0:1, :], lanec[1:2, :], lanec[2:3, :]
    x0, x1, x2 = xv[0:1, 0:1], xv[1:2, 0:1], xv[2:3, 0:1]
    along = x0 * cosphi + x1 * sinphi
    across = x1 * cosphi - x0 * sinphi
    for i in range(nlat):
        sl = slice(i * 5 * ROWS, (i + 1) * 5 * ROWS)
        ca, cc, cz, at = (rowc[sl, j : j + 1] for j in range(4))
        rigid = ca * along + cc * across + cz * x2
        weighted = (grid[:, i * fs : (i + 1) * fs] - rigid) * at * wphi
        hat[sl, :] = jnp.dot(
            weighted, circle[...], precision=highest, preferred_element_type=f32
        )
    blocks = degrees // ROWS
    spots = [(i, b, y) for i in range(nlat) for b in range(5) for y in range(ny)]
    zero = jnp.zeros((ROWS, degrees), f32)

    def rows_of(ref, i, b, y, k, part):
        r = (i * 5 + b) * ROWS + k * ny + y
        return ref[r : r + 1, part * degrees : (part + 1) * degrees]

    base = [lat_of(i, nlat) * (5 * ny) for i in range(nlat)]

    def analyse(blk, carry):
        l0 = pl.multiple_of(blk * (2 * ROWS), 2 * ROWS)
        accs = [[zero] * 6 for _ in range(2)]
        for i, b, y in spots:
            t = base[i] + y * 5 + b
            p = [legendre[t, pl.ds(l0 + h * ROWS, ROWS), :] for h in range(2)]
            for k in range(3):
                for part in range(2):
                    value = rows_of(hat, i, b, y, k, part)
                    for h in range(2):
                        accs[h][k * 2 + part] = accs[h][k * 2 + part] + p[h] * value
        for h in range(2):
            sl = pl.ds(l0 + h * ROWS, ROWS)
            for kp in range(6):
                coef_out[kp, sl, :] = accs[h][kp]
            for k in range(3):
                for part in range(2):
                    total = zero
                    for s, ref in enumerate([None] + coef_refs):
                        for m in range(3):
                            value = accs[h][m * 2 + part] if s == 0 else ref[m * 2 + part, sl, :]
                            col = (s * 3 + k) * 3 + m
                            total = total + kern[sl, col : col + 1] * value
                    state[k * 2 + part, sl, :] = total
        return carry

    lax.fori_loop(0, blocks // 2, analyse, 0)
    ids = row_ids((ROWS, degrees))
    for i in range(nlat):

        def synth(b, carry, i=i):
            accs = [[zero] * 6 for _ in range(ny)]
            for blk in range(blocks):
                sl = slice(blk * ROWS, (blk + 1) * ROWS)
                held = [state[kp, sl, :] for kp in range(6)]
                for y in range(ny):
                    p = legendre[base[i] + y * 5 + b, sl, :]
                    for kp in range(6):
                        accs[y][kp] = accs[y][kp] + p * held[kp]
            for part in range(2):
                block = zero
                for k in range(3):
                    for y in range(ny):
                        row = jnp.sum(accs[y][k * 2 + part], axis=0, keepdims=True)
                        block = jnp.where(ids == k * ny + y, row, block)
                shat[
                    pl.ds(pl.multiple_of((i * 5 + b) * ROWS, ROWS), ROWS),
                    part * degrees : (part + 1) * degrees,
                ] = block
            return carry

        lax.fori_loop(0, 5, synth, 0)
    traction = lax.dot_general(
        shat[...],
        circle[...],
        (((1,), (1,)), ((), ())),
        precision=highest,
        preferred_element_type=f32,
    )
    count = nlat * 5 * ROWS
    earlier = [
        hist[pl.ds(pl.multiple_of(n * count + lat_of(i, nlat) * (5 * ROWS), ROWS), 5 * ROWS), :]
        for i in range(nlat)
    ]
    traction = traction + jnp.concatenate(earlier, axis=0)
    out[...] = traction
    ca, cc, cz, at = (rowc[:, j : j + 1] for j in range(4))
    weighted = traction * at * wphi
    radial = jnp.sum(weighted * ca, axis=0, keepdims=True)
    turning = jnp.sum(weighted * cc, axis=0, keepdims=True)
    polar = jnp.sum(weighted * cz, axis=0, keepdims=True)
    pulls = [
        jnp.sum(radial * cosphi - turning * sinphi, axis=1, keepdims=True),
        jnp.sum(radial * sinphi + turning * cosphi, axis=1, keepdims=True),
        jnp.sum(polar, axis=1, keepdims=True),
    ]
    for j in range(3):
        speed = xv[3 + j : 4 + j, :] + time_step * rigid_gain * pulls[j]
        xv_out[3 + j : 4 + j, :] = speed
        xv_out[j : j + 1, :] = xv[j : j + 1, :] + time_step * speed
    xv_out[6:8, :] = jnp.zeros((2, xv_out.shape[1]), f32)


def first_interface(dims, npieces, *refs):
    ny, nlat, nblk, lanes = dims
    pieces = refs[:npieces]
    tables, order_circle, xv = refs[npieces : npieces + 5], refs[npieces + 5], refs[npieces + 6]
    u, hist, coef, xv_out, out = refs[npieces + 7 : npieces + 12]
    rows_ref, held, state, hat, shat = refs[npieces + 12 :]
    unpack(pieces, 0, rows_ref, u, dims)
    at = 0
    for ref in pieces:
        for d in range(ref.shape[0] // PAY):
            for q in range(HEAD // ROWS):
                held[at : at + ROWS, q * 128 : (q + 1) * 128] = ref[
                    d * PAY + q * ROWS : d * PAY + (q + 1) * ROWS, :
                ]
            at += ROWS
    hist[...] = lax.dot_general(
        held[:, 0 : hist.shape[0]],
        order_circle[...],
        (((0,), (0,)), ((), ())),
        precision=highest,
        preferred_element_type=f32,
    )
    to_traction(dims, 0, u, tables, state, xv, hist, [], coef, hat, shat, xv_out, out)


def interface_force(dims, u, aux, scaled, force):
    ny, nlat, nblk, lanes = dims
    count = nlat * nblk
    stiffness(u, scaled, force, aux, ny)
    join_rows(force, ny)
    shape = (ROWS, lanes)
    lam = lane_ids(shape)
    rows = row_ids(shape)
    y = rows % ny
    lat_at = lax.rem(lam, nlat)
    blk_at = lax.rem(lax.div(lam, nlat), nblk)
    for ab in range(25):
        high = ab * 5 + 4
        force[high] = force[high] + jnp.where(
            lam < count, pltpu.roll(force[ab * 5], lanes - count, 1), 0.0
        )
    wrap = count - nlat
    for bc in range(25):
        first, last = force[bc], force[100 + bc]
        lower = jnp.where(
            blk_at == 0, pltpu.roll(last, lanes - wrap, 1), pltpu.roll(last, nlat, 1)
        )
        upper = jnp.where(
            blk_at == nblk - 1, pltpu.roll(first, wrap, 1), pltpu.roll(first, lanes - nlat, 1)
        )
        force[bc] = first + lower
        force[100 + bc] = last + upper
    absolute = lax.rem(lat_at + lax.axis_index("lat"), nlat)
    take_low = jnp.logical_and(y == 0, absolute > 0)
    take_high = jnp.logical_and(y == ny - 1, absolute < nlat - 1)
    for a in range(5):
        for c in range(5):
            low, high = a * 25 + c, a * 25 + 20 + c
            first, last = force[low], force[high]
            lower = jnp.where(
                lat_at == 0, pltpu.roll(last, lanes - (nlat - 1), 1), pltpu.roll(last, 1, 1)
            )
            upper = jnp.where(
                lat_at == nlat - 1, pltpu.roll(first, nlat - 1, 1), pltpu.roll(first, lanes - 1, 1)
            )
            force[low] = first + jnp.where(
                take_low, pltpu.roll(lower, ROWS - (ny - 1), 0), 0.0
            )
            force[high] = last + jnp.where(take_high, pltpu.roll(upper, ny - 1, 0), 0.0)


def add_traction(dims, traction, force, fs):
    ny, nlat, nblk, lanes = dims
    shape = (ROWS, lanes)
    lam = lane_ids(shape)
    rows = row_ids(shape)
    absolute = lax.rem(lax.rem(lam, nlat) + lax.axis_index("lat"), nlat)
    y = rows % ny
    grid = jnp.concatenate(
        [traction[i * 5 * ROWS : (i + 1) * 5 * ROWS, :] for i in range(nlat)], axis=1
    )
    parts = split3(grid)
    for a in range(5):
        place = place_matrix(a, dims, fs)
        moved = jnp.zeros((5 * ROWS, lanes), f32)
        for piece in parts:
            moved = moved + lax.dot_general(
                piece, place, (((1,), (1,)), ((), ())), preferred_element_type=f32
            )
        wa = float(WEIGHTS[a] * (2.0 if a in (0, 4) else 1.0))
        for b in range(5):
            weight = float(WEIGHTS[b]) * wa
            if b == 0:
                shared = jnp.logical_or(y > 0, absolute > 0)
            elif b == 4:
                shared = jnp.logical_or(y < ny - 1, absolute < nlat - 1)
            else:
                shared = None
            face = weight if shared is None else jnp.where(shared, 2.0 * weight, weight)
            at = a * 25 + b * 5
            force[at] = force[at] - face * moved[b * ROWS : (b + 1) * ROWS]


def second_interface(dims, npieces, *refs):
    ny, nlat, nblk, lanes = dims
    pieces = refs[:npieces]
    tables = refs[npieces : npieces + 5]
    xv, hist, u, coef0, traction = refs[npieces + 5 : npieces + 10]
    new_u, new_v, inverse, coef, xv_out, out = refs[npieces + 10 : npieces + 16]
    rows_ref, state, hat, shat, force, scaled, v = refs[npieces + 16 :]
    unpack(pieces, 1, rows_ref, v, dims)
    interface_force(dims, u, v, scaled, force)
    rows = row_ids((ROWS, lanes))
    lam = lane_ids((ROWS, lanes))
    for node in range(N3):
        mass = force[node]
        inverse[node] = spread_inverse(jnp.where(lam < nlat * nblk, mass, 1.0), ny)
    add_traction(dims, traction, force, tables[1].shape[0])
    for node in range(N3):
        speed = v[node] + time_step * force[node] * inverse[node]
        new_v[node] = speed
        new_u[node] = jnp.where(rows < 3 * ny, u[node] + time_step * speed, u[node])
    to_traction(dims, 1, new_u, tables, state, xv, hist, [coef0], coef, hat, shat, xv_out, out)


def third_interface(dims, *refs):
    ny, nlat, nblk, lanes = dims
    tables = refs[:5]
    xv, hist, u, v, inverse, coef1, coef0, traction, owner = refs[5:14]
    xv_out, out, kept = refs[14:17]
    state, hat, shat, force, scaled, coef = refs[17:]
    interface_force(dims, u, None, scaled, force)
    add_traction(dims, traction, force, tables[1].shape[0])
    rows = row_ids((ROWS, lanes))
    for ab in range(25):
        node = ab * 5
        speed = v[node] + time_step * force[node] * inverse[node]
        scaled[node] = u[node] + time_step * speed
    to_traction(
        dims, 2, scaled, tables, state, xv, hist, [coef1, coef0], coef, hat, shat, xv_out, out
    )
    nown = kept.shape[0]
    degrees = tables[0].shape[-1]
    device = lax.axis_index("blk") * nlat + lax.axis_index("lat")
    ids = row_ids((ROWS, 2 * degrees))
    column = jnp.full((ROWS, 2 * degrees), -1, jnp.int32)
    for j in range(nown):
        column = jnp.where(ids == j, owner[device * nown + j], column)
    hot = jnp.where(column == lane_ids((ROWS, 2 * degrees)), 1.0, 0.0)
    for n, ref in enumerate((coef, coef1, coef0)):
        for k in range(3):
            both = jnp.concatenate([ref[2 * k], ref[2 * k + 1]], axis=1)
            mine = lax.dot_general(
                hot, both, (((1,), (1,)), ((), ())), precision=highest, preferred_element_type=f32
            )
            for j in range(nown):
                kept[j, n, k : k + 1, :] = mine[j : j + 1]


def legendre_tables(colatitude, degrees):
    cosine = np.cos(colatitude)[:, None]
    sine = np.sin(colatitude)[:, None]
    orders = np.arange(degrees, dtype=np.float64)[None, :]
    factor = np.where(
        orders == 0,
        math.sqrt(0.5),
        -np.sqrt((2.0 * orders + 1.0) / np.maximum(2.0 * orders, 1.0)) * sine,
    )
    diagonal = np.cumprod(factor, axis=1)
    levels = np.zeros((len(colatitude), degrees, degrees))
    ups = np.zeros((degrees, degrees))
    downs = np.zeros((degrees, degrees))
    previous = before = np.zeros((len(colatitude), degrees))
    for level in range(degrees):
        above = orders < level
        up = np.where(
            above,
            np.sqrt(
                max(4.0 * level * level - 1.0, 0.0) / np.maximum(level * level - orders**2, 1.0)
            ),
            0.0,
        )
        lowered = (level - 1.0) ** 2
        down = np.where(
            above,
            np.sqrt(np.maximum(lowered - orders**2, 0.0) / max(4.0 * lowered - 1.0, 1.0)),
            0.0,
        )
        values = up * (cosine * previous - down * before)
        values = np.where(orders == level, diagonal, values)
        levels[:, level, :] = values
        ups[level], downs[level] = up[0], down[0]
        before, previous = previous, values
    return (
        levels.astype(np.float32),
        ups.astype(np.float32),
        downs.astype(np.float32),
        diagonal.astype(np.float32),
    )


def on_device(
    mesh_sizes,
    displacement,
    velocity,
    rigidity,
    density,
    history,
    kernel,
    owner_order,
    rigid_offset,
    rigid_velocity,
):
    nblk, nlat = mesh_sizes
    nx, ny, depth = displacement.shape[4:]
    assert nx == 1 and 4 * ny == ROWS
    degrees = kernel.shape[3]
    lags = kernel.shape[0]
    nown = history.shape[0]
    lat_elems, lon_elems = ny * nlat, nblk
    nt, nf = 5 * lat_elems, 5 * lon_elems
    count = nblk * nlat
    lanes = -(-2 * count // 128) * 128
    fs = -(-nf // 128) * 128
    rows_all = nlat * 5 * ROWS
    dims = (ny, nlat, nblk, lanes)
    blk, lat = lax.axis_index("blk"), lax.axis_index("lat")

    theta_step = (math.pi - 2.0 * pole_gap) / lat_elems
    phi_step = 2.0 * math.pi / lon_elems
    theta = pole_gap + (np.arange(nt) // 5 + 0.5 * (1.0 + np.tile(POINTS, lat_elems))) * theta_step
    phi = (np.arange(nf) // 5 + 0.5 * (1.0 + np.tile(POINTS, lon_elems))) * phi_step
    table, ups, downs, diagonal = legendre_tables(theta, degrees)
    orders = np.arange(degrees)[None, :]
    angles = phi[:, None] * orders
    cosines = np.where(orders == 0, 1.0 / math.sqrt(2.0 * math.pi), np.cos(angles) / math.sqrt(math.pi))
    sines = np.where(orders == 0, 0.0, np.sin(angles) / math.sqrt(math.pi))
    circle_all = np.concatenate([cosines, sines], axis=1).astype(np.float32)
    r = np.arange(rows_all)
    r_lat, r_b, r_s = r // (5 * ROWS), (r // ROWS) % 5, r % ROWS
    r_k, r_y = r_s // ny, r_s % ny
    r_t = (r_lat * ny + r_y) * 5 + r_b
    real = r_k < 3
    th = theta[r_t]
    rowc_all = np.zeros((rows_all, 8))
    rowc_all[:, 0] = np.where(r_k == 0, np.sin(th), np.where(r_k == 1, np.cos(th), 0.0))
    rowc_all[:, 1] = np.where(r_k == 2, 1.0, 0.0)
    rowc_all[:, 2] = np.where(r_k == 0, np.cos(th), np.where(r_k == 1, -np.sin(th), 0.0))
    rowc_all[:, 3] = np.where(
        real, 0.25 * theta_step * phi_step * WEIGHTS[r_b] * np.sin(th), 0.0
    )
    lanec_all = np.zeros((8, nf))
    lanec_all[0], lanec_all[1] = np.cos(phi), np.sin(phi)
    lanec_all[2] = np.tile(WEIGHTS, lon_elems)
    diag_rows = np.where(real[:, None], diagonal[r_t], 0.0).astype(np.float32)
    cos_rows = np.where(real, np.cos(th), 0.0).astype(np.float32)

    def rolled(values, start, axis):
        both = jnp.asarray(np.concatenate([values, values], axis=axis).astype(np.float32))
        return lax.dynamic_slice_in_dim(both, start, values.shape[axis], axis)

    vmem = pl.BlockSpec(memory_space=pltpu.VMEM)
    smem = pl.BlockSpec(memory_space=pltpu.SMEM)
    def shaped(*dims_):
        return jax.ShapeDtypeStruct(dims_, f32)

    def cost(micros):
        return pl.CostEstimate(
            flops=int(micros * 5e6), transcendentals=0, bytes_accessed=int(micros * 1e6)
        )

    u4 = displacement.reshape(3, N3, ny, depth)
    v4 = velocity.reshape(3, N3, ny, depth)
    rig = rigidity.reshape(N3, ny, depth)
    dens = density.reshape(N3, ny, depth)

    payload = pl.pallas_call(
        functools.partial(gather_kernel, (ny, nlat, nown, rows_all, degrees)),
        out_shape=shaped(PAY, 128),
        in_specs=[vmem] * 10 + [smem],
        out_specs=vmem,
        scratch_shapes=[pltpu.VMEM((N3, ROWS, depth), f32)] * 2
        + [pltpu.VMEM((ROWS, 16 * HEAD), f32)],
        name="gather",
        cost_estimate=cost(6),
    )(
        u4,
        v4,
        rig,
        dens,
        history,
        kernel,
        jnp.asarray(ups),
        jnp.asarray(downs),
        jnp.asarray(diag_rows),
        jnp.asarray(np.tile(cos_rows[None], (8, 1))),
        owner_order,
    )

    def shifted(x, axis, size, by):
        return lax.ppermute(x, axis, [(s, (s - by) % size) for s in range(size)])

    column = jnp.concatenate(
        [payload] + [shifted(payload, "lat", nlat, i) for i in range(1, nlat)], axis=0
    )
    if nblk <= 8:
        pieces = [column] + [shifted(column, "blk", nblk, i) for i in range(1, nblk)]
        base_blk = blk
    else:
        pieces = [lax.all_gather(column, "blk", axis=0, tiled=True)]
        base_blk = blk * 0

    packed = shaped(N3, ROWS, depth)
    face = shaped(25, ROWS, depth)
    buffer = pltpu.VMEM((N3, ROWS, depth), f32)
    pu, pv, force, *faces = pl.pallas_call(
        functools.partial(start_kernel, ny),
        out_shape=(packed,) * 3 + (face,) * 4,
        in_specs=[vmem] * 4,
        out_specs=(vmem,) * 7,
        scratch_shapes=[buffer],
        name="forces",
        cost_estimate=cost(4),
    )(u4, v4, rig, dens)

    def exchange(left, right, low, high):
        from_left = shifted(right, "blk", nblk, -1)
        from_right = shifted(left, "blk", nblk, 1)
        low = jnp.concatenate([low[:5] + from_left[:5], low[5:20], low[20:] + from_right[:5]])
        high = jnp.concatenate([high[:5] + from_left[20:], high[5:20], high[20:] + from_right[20:]])
        return from_left, from_right, shifted(high, "lat", nlat, -1), shifted(low, "lat", nlat, 1)

    circle = rolled(circle_all, base_blk * 5, 0)
    circle = jnp.pad(circle, ((0, fs - nf), (0, 0)))
    lanec = jnp.pad(rolled(lanec_all, base_blk * 5, 1), ((0, 0), (0, fs - nf)))
    rowc = rolled(rowc_all, lat * (5 * ROWS), 0)
    owners = owner_order.reshape(nblk, nlat, nown)
    owners = lax.dynamic_slice_in_dim(jnp.concatenate([owners, owners], 0), base_blk, nblk, 0)
    owners = lax.dynamic_slice_in_dim(jnp.concatenate([owners, owners], 1), lat, nlat, 1)
    owners = jnp.pad(owners.reshape(count, nown), ((0, 0), (0, ROWS - nown)), constant_values=-1)
    owners = owners.reshape(count * ROWS)
    hot = (owners[:, None] == jnp.arange(2 * degrees, dtype=jnp.int32)[None, :]).astype(f32)
    order_circle = jnp.einsum("pc,fc->pf", hot, circle, precision=highest)
    kern = kernel[:3].reshape(27, degrees).T
    tables = (jnp.asarray(table), circle, rowc, lanec, kern)
    xv = jnp.concatenate([rigid_offset, rigid_velocity, jnp.zeros((2,), f32)])
    xv = jnp.broadcast_to(xv[:, None], (8, 128))

    wide = shaped(N3, ROWS, lanes)
    held = pltpu.VMEM((N3, ROWS, lanes), f32)
    coefs = shaped(6, degrees, degrees)
    grid_rows = shaped(rows_all, fs)
    hats = [
        pltpu.VMEM((6, degrees, degrees), f32),
        pltpu.VMEM((rows_all, 2 * degrees), f32),
        pltpu.VMEM((rows_all, 2 * degrees), f32),
    ]
    npieces = len(pieces)
    xvs = shaped(8, 128)
    gu, hist, coef0, xv1, traction0 = pl.pallas_call(
        functools.partial(first_interface, dims, npieces),
        out_shape=(wide, shaped(3 * rows_all, fs), coefs, xvs, grid_rows),
        in_specs=[vmem] * (npieces + 7),
        out_specs=(vmem,) * 5,
        scratch_shapes=[pltpu.VMEM((CHUNKS, lanes, 128), f32), pltpu.VMEM((count * ROWS, 16 * HEAD), f32)]
        + hats,
        name="interface0",
        cost_estimate=cost(8),
    )(*pieces, *tables, order_circle, xv)

    def own(traction):
        mine = traction[: 5 * ROWS]
        if nblk > 8:
            mine = lax.dynamic_slice_in_dim(mine, blk * 5, 5, 1)
            mine = jnp.pad(mine, ((0, 0), (0, depth - 5)))
        return mine

    def advance(first, last, force, moved, traction, pu, pv, inverse):
        three = shaped(3, N3, ny, depth)
        outs = (three,) * 2 if last else (packed,) * 3 + (face,) * 4 + (packed,) * first
        return pl.pallas_call(
            functools.partial(advance_kernel, (ny, nlat, depth), first, last),
            out_shape=outs,
            in_specs=[vmem] * (8 + (not first)),
            out_specs=(vmem,) * len(outs),
            scratch_shapes=[buffer] * (1 if last and not first else 2),
            name="advance",
            cost_estimate=cost(4),
        )(force, *moved, own(traction), pu, pv, *(() if first else (inverse,)))

    moved = exchange(*faces)
    pu, pv, force, *rest = advance(True, False, force, moved, traction0, pu, pv, None)
    faces, inverse = rest[:4], rest[4]
    moved = exchange(*faces)
    gu1, gv1, ginv, coef1, xv2, traction1 = pl.pallas_call(
        functools.partial(second_interface, dims, npieces),
        out_shape=(wide, wide, wide, coefs, xvs, grid_rows),
        in_specs=[vmem] * (npieces + 10),
        out_specs=(vmem,) * 6,
        scratch_shapes=[pltpu.VMEM((CHUNKS, lanes, 128), f32)] + hats + [held] * 3,
        name="interface1",
        cost_estimate=cost(8),
    )(*pieces, *tables, xv1, hist, gu, coef0, traction0)
    pu, pv, force, *faces = advance(False, False, force, moved, traction1, pu, pv, inverse)
    moved = exchange(*faces)
    xv3, traction2, kept = pl.pallas_call(
        functools.partial(third_interface, dims),
        out_shape=(xvs, grid_rows, shaped(nown, 3, 3, degrees)),
        in_specs=[vmem] * 13 + [smem],
        out_specs=(vmem,) * 3,
        scratch_shapes=hats + [held] * 2 + [pltpu.VMEM((6, degrees, degrees), f32)],
        name="interface2",
        cost_estimate=cost(8),
    )(*tables, xv2, hist, gu1, gv1, ginv, coef1, coef0, traction1, owner_order)
    new_u, new_v = advance(False, True, force, moved, traction2, pu, pv, inverse)
    new_history = jnp.concatenate([kept, history[:, : lags - 1 - STEPS]], axis=1)
    return (
        new_u.reshape(displacement.shape),
        new_v.reshape(velocity.shape),
        new_history,
        xv3[0:3, 0],
        xv3[3:6, 0],
    )


def solution(mesh):
    field = P(None, None, None, None, "blk", "lat", None)
    nodal = P(None, None, None, "blk", "lat", None)
    columns = P(("blk", "lat"), None, None, None)
    in_specs = (field, field, nodal, nodal, columns, P(), P(), P(), P())
    out_specs = (field, field, columns, P(), P())
    return jax.shard_map(
        functools.partial(on_device, (mesh.shape["blk"], mesh.shape["lat"])),
        mesh=mesh,
        in_specs=in_specs,
        out_specs=out_specs,
        check_vma=False,
    )
```

time: 934 us -> 129 us (0.14)
  blocking collectives: 269 us -> 0 us
  local copies, waits for them, and re-layouts: 184 us -> 21.3 us
  other arithmetic: 138 us -> 4.42 us
  waiting for transfers between devices: 123 us -> 18.3 us
  loops' own time: 88.9 us -> 0 us
  matrix products: 63.1 us -> 0.97 us
  Pallas kernels: 0 us -> 50.1 us
  between operations: 16.3 us -> 0.93 us
  starting transfers between devices: 42 us -> 31.5 us
    all_gather x3 -> x0, blocking collectives: 123 us -> none  [on_device(): gathered = lax.all_gather(replies, ('blk', 'lat'), axis=0, tiled=True)]
    psum x3 -> x0, blocking collectives: 108 us -> none  [on_device(): lax.psum(jnp.einsum('jktf,ktf->j', rotated * area_weight, traction, preci...]
    unnamed x6 -> x0, waiting for transfers between devices: 104 us -> none
    another operation x1 -> x0, loops' own time: 88.9 us -> none  [legendre(): lax.scan(advance, (zeroed, zeroed), jnp.arange(degrees, dtype=jnp.int32))]
    dynamic_update_slice x128 -> x0, other arithmetic: 86.7 us -> none  [legendre(): lax.scan(advance, (zeroed, zeroed), jnp.arange(degrees, dtype=jnp.int32))]
    dynamic_slice x128 -> x3, local copies, waits for them, and re-layouts: 74.5 us -> 0.72 us  [rolled(): return lax.dynamic_slice_in_dim(both, start, values.shape[axis], axis)]
    dot_general x39 -> x1, matrix products: 63.1 us -> 0.97 us  [on_device(): order_circle = jnp.einsum('pc,fc->pf', hot, circle, precision=highest)]
    pallas_call x0 -> x8, Pallas kernels: none -> 50.1 us  [the longest x3 11 us: advance(): pl.pallas_call(functools.partial(advance_kernel, (ny, nlat, depth), first...]
  transfers between devices with their start and end apart: 19 -> 22, of which waited for: 8 -> 6; matrix products, arithmetic and copies ran while one was open for 27% -> 14% of each run, Pallas kernels for 0% -> 24%
where the time goes in v1:
time: 129 us; the launch traced here: 128 us
  Pallas kernels  50.1 us (39%)
  starting transfers between devices  31.5 us (24%)
  local copies, waits for them, and re-layouts  21.3 us (17%)
  waiting for transfers between devices  18.3 us (14%)
  other arithmetic  4.42 us (3%)
    ppermute x22, starting transfers between devices, shifted(): return lax.ppermute(x, axis, [(s, (s - by) % size) for s in range(size)])  31.5 us
    ppermute x22, waiting for transfers between devices, shifted(): return lax.ppermute(x, axis, [(s, (s - by) % size) for s in range(size)])  18.3 us
    pallas_call x3, Pallas kernels, advance(): pl.pallas_call(functools.partial(advance_kernel, (ny, nlat, depth), first...  11 us
    pallas_call x1, Pallas kernels, on_device(): pl.pallas_call(functools.partial(third_interface, dims), out_shape=(xvs,...  10.2 us
    pallas_call x1, Pallas kernels, on_device(): pl.pallas_call(functools.partial(second_interface, dims, npieces), out_sh...  9.5 us
    pallas_call x1, Pallas kernels, on_device(): pl.pallas_call(functools.partial(gather_kernel, (ny, nlat, nown, rows_all...  8.08 us
    pallas_call x1, Pallas kernels, on_device(): pl.pallas_call(functools.partial(first_interface, dims, npieces), out_sha...  7.71 us
    unnamed x56, local copies, waits for them, and re-layouts  6.43 us
  transfers between devices with their start and end apart: 22, of which 6 were waited for; matrix products, arithmetic and copies ran while one was open for 14% of the time, Pallas kernels for 24%

profile of v1, /device:TPU:1, one launch (start us, length us, event | category | flops | bytes accessed | tf_op | source)
XLA Modules:
  0.0 127.5 jit_solution(8145705219806546297)
XLA Ops:
  0.6 2.4 %copy.28.hist = f32[8,63,3,128]{3,2,1,0:T(4,128)} copy(f32[8,63,3,128]{3,0,2,1:T(8,128)} %param.21) | data formatting | bytes 1548288 | tf_op args[4]
  3.0 2.0 %copy.29.kern = f32[64,3,3,128]{3,2,1,0:T(4,128)} copy(f32[64,3,3,128]{3,0,2,1:T(8,128)} %param.22) | data formatting | bytes 589824 | tf_op args[5]
  5.0 8.1 %gather.1 = f32[64,128]{1,0:T(8,128)} custom-call(f32[3,125,2,128]{3,2,1,0:T(2,128)} %bitcast.11, f32[3,125,2,128]{3,2,1,0:T(2,128)} %bitcast.13, f32[125,2,128]{2,1,0:T(2,128)} %bitcast.18, f32[125,2,128]{2,1,0:T(2,128)} %bitcast.20, f32[8,63,3,128]{3,2,1,0:T(4,128)} %copy.28.hist, f32[64,3,3,128]{3,2,1,0:T(4,128)} %copy.29.kern, ...), custom_call_target="tpu_custom_call" | custom-call | flops 30000000 | bytes 6000000 | tf_op jit(solution)/shard_map/gather/pallas_call | solution.py:783
  13.1 2.7 %collective-permute-start.5 = (f32[64,128]{1,0:T(8,128)}, f32[64,128]{1,0:T(8,128)S(1)}, u32[]{:S(2)}, u32[]{:S(2)}) collective-permute-start(f32[64,128]{1,0:T(8,128)} %gather.1), channel_id=1, source_target_pairs={{0,2},{1,3},{2,0},{3,1},{4,6},{5,7},{6,4},{7,5},{8,10},{9,11},{10,... | collective-permute-start | bytes 98312 | tf_op jit(solution)/shard_map/ppermute | solution.py:807
  15.8 1.4 %collective-permute-start.6 = (f32[64,128]{1,0:T(8,128)}, f32[64,128]{1,0:T(8,128)S(1)}, u32[]{:S(2)}, u32[]{:S(2)}) collective-permute-start(f32[64,128]{1,0:T(8,128)} %gather.1), channel_id=1, source_target_pairs={{0,1},{1,2},{2,3},{3,0},{4,5},{5,6},{6,7},{7,4},{8,9},{9,10},{10,1... | collective-permute-start | bytes 98312 | tf_op jit(solution)/shard_map/ppermute | solution.py:807
  17.2 3.6 %forces.1 = (f32[125,8,128]{2,1,0:T(8,128)}, f32[125,8,128]{2,1,0:T(8,128)}, f32[125,8,128]{2,1,0:T(8,128)}, f32[25,8,128]{2,1,0:T(8,128)}, f32[25,8,128]{2,1,0:...) custom-call(f32[3,125,2,128]{3,2,1,0:T(2,128)} %bitcast.12, f32[3,125,2,128]{3,2,1,0:T(2,128)} %bitcast.14, ...), custom_call_target="tpu_custom_call" | custom-call | flops 20000000 | bytes 4000000 | tf_op jit(solution)/shard_map/forces/pallas_call | solution.py:822
  20.8 1.2 collective-permute-start
  22.0 3.1 %collective-permute-start.1 = (f32[25,8,128]{2,1,0:T(8,128)}, f32[25,8,128]{2,1,0:T(8,128)S(1)}, u32[]{:S(2)}, u32[]{:S(2)}) collective-permute-start(f32[25,8,128]{2,1,0:T(8,128)} %get-tuple-element.45), channel_id=1, source_target_pairs={{0,28},{4,0},{8,4},{12,8},{16,12},{20,16},{24,20},{28,24},{1,29},{... | collective-permute-start | bytes 307208 | tf_op jit(solution)/shard_map/ppermute | solution.py:807
  25.1 0.1 reshape.43
  25.3 0.1 eq.15
  25.4 1.0 fusion.refs_13_
  26.4 0.6 constant_dynamic-slice_fusion.1.refs_10_.refs_2_
  27.1 0.1 constant_dynamic-slice_fusion
  27.1 0.8 slice.121
  27.9 0.7 pad.8.refs_9_.refs_1_
  28.6 0.6 pad.9.refs_11_.refs_3_
  29.2 0.7 copy.31
  29.9 0.8 slice.118
  30.8 0.8 slice.113
  31.6 0.8 pad_maximum_fusion.1.refs_0_
  32.4 0.4 collective-permute-start.10
  32.8 1.3 %collective-permute-start.11 = (f32[256,128]{1,0:T(8,128)S(1)}, f32[256,128]{1,0:T(8,128)S(1)}, u32[]{:S(2)}, u32[]{:S(2)}) collective-permute-start(f32[256,128]{1,0:T(8,128)S(1)} %pad_maximum_fusion.1.refs_0_), channel_id=1, source_target_pairs={{0,12},{4,16},{8,20},{12,24},{16,28},{20,0},{24,4},{28,8},{1,13},{... | collective-permute-start | bytes 393224 | tf_op jit(solution)/shard_map/ppermute | solution.py:807
  34.2 1.9 %collective-permute-start.13 = (f32[256,128]{1,0:T(8,128)S(1)}, f32[256,128]{1,0:T(8,128)S(1)}, u32[]{:S(2)}, u32[]{:S(2)}) collective-permute-start(f32[256,128]{1,0:T(8,128)S(1)} %pad_maximum_fusion.1.refs_0_), channel_id=1, source_target_pairs={{0,4},{4,8},{8,12},{12,16},{16,20},{20,24},{24,28},{28,0},{1,5},{5... | collective-permute-start | bytes 393224 | tf_op jit(solution)/shard_map/ppermute | solution.py:807
  36.1 3.0 %collective-permute-start.7 = (f32[256,128]{1,0:T(8,128)S(1)}, f32[256,128]{1,0:T(8,128)S(1)}, u32[]{:S(2)}, u32[]{:S(2)}) collective-permute-start(f32[256,128]{1,0:T(8,128)S(1)} %pad_maximum_fusion.1.refs_0_), channel_id=1, source_target_pairs={{0,28},{4,0},{8,4},{12,8},{16,12},{20,16},{24,20},{28,24},{1,29},{... | collective-permute-start | bytes 393224 | tf_op jit(solution)/shard_map/ppermute | solution.py:807
  39.1 0.8 slice_add_fusion.9
  39.9 6.6 %collective-permute-done.10.refs_4_ = f32[256,128]{1,0:T(8,128)S(1)} collective-permute-done((f32[256,128]{1,0:T(8,128)S(1)}, f32[256,128]{1,0:T(8,128)S(1)}, u32[]{:S(2)}, u32[]{:S(2)}) %collective-permute-start.10) | collective-permute-done | bytes 131104 | tf_op jit(solution)/shard_map/ppermute | solution.py:807
  46.5 4.4 %collective-permute-done.11.refs_5_ = f32[256,128]{1,0:T(8,128)S(1)} collective-permute-done((f32[256,128]{1,0:T(8,128)S(1)}, f32[256,128]{1,0:T(8,128)S(1)}, u32[]{:S(2)}, u32[]{:S(2)}) %collective-permute-start.11) | collective-permute-done | bytes 131104 | tf_op jit(solution)/shard_map/ppermute | solution.py:807
  50.9 0.8 collective-permute-start.3
  51.7 1.0 collective-permute-start.2
  52.7 0.1 pad_maximum_fusion.8
  52.8 3.3 %collective-permute-done.9.refs_3_ = f32[256,128]{1,0:T(8,128)S(1)} collective-permute-done((f32[256,128]{1,0:T(8,128)S(1)}, f32[256,128]{1,0:T(8,128)S(1)}, u32[]{:S(2)}, u32[]{:S(2)}) %collective-permute-start.9) | collective-permute-done | bytes 131104 | tf_op jit(solution)/shard_map/ppermute | solution.py:807
  56.0 0.7 broadcast_in_dim.2.refs_14_
  56.7 7.7 %interface0.1 = (f32[125,8,128]{2,1,0:T(8,128)}, f32[480,128]{1,0:T(8,128)}, f32[6,128,128]{2,1,0:T(8,128)}, f32[8,128]{1,0:T(8,128)}, f32[160,128]{1,0:T(8,128)}) custom-call(f32[256,128]{1,0:T(8,128)} %copy-done, f32[256,128]{1,0:T(8,128)} %copy-done.5, f32[256,128]{1,0:T(8,128)} %copy-done.6, f32[256,128]{1,0:T(8,128)} %copy-done.7, ...), custom_call_target="tpu_custom_call" | custom-call | flops 40000000 | bytes 8000000 | tf_op jit(solution)/shard_map/interface0/pallas_call | solution.py:866
  64.5 1.3 %slice.122.refs_5_ = f32[40,128]{1,0:T(8,128)} slice(f32[160,128]{1,0:T(8,128)} %get-tuple-element.48.refs_17_), slice={[0:40], [0:128]} | slice | bytes 40960 | tf_op jit(solution)/shard_map/slice | solution.py:878
  65.8 0.6 copy-done.18
  66.4 0.1 copy-done.19
  66.5 4.1 %advance.3 = (f32[125,8,128]{2,1,0:T(8,128)}, f32[125,8,128]{2,1,0:T(8,128)}, f32[125,8,128]{2,1,0:T(8,128)}, f32[25,8,128]{2,1,0:T(8,128)}, f32[25,8,128]{2,1,0...) custom-call(f32[125,8,128]{2,1,0:T(8,128)} %get-tuple-element.43.refs_0_, ...), custom_call_target="tpu_custom_call" | custom-call | flops 20000000 | bytes 4000000 | tf_op jit(solution)/shard_map/advance/pallas_call | solution.py:887
  70.6 2.1 %collective-permute-start.14 = (f32[25,8,128]{2,1,0:T(8,128)}, f32[25,8,128]{2,1,0:T(8,128)S(1)}, u32[]{:S(2)}, u32[]{:S(2)}) collective-permute-start(f32[25,8,128]{2,1,0:T(8,128)} %get-tuple-element.52), channel_id=1, source_target_pairs={{0,4},{4,8},{8,12},{12,16},{16,20},{20,24},{24,28},{28,0},{1,5},{5... | collective-permute-start | bytes 307208 | tf_op jit(solution)/shard_map/ppermute | solution.py:807
  72.7 2.7 %collective-permute-start.15 = (f32[25,8,128]{2,1,0:T(8,128)}, f32[25,8,128]{2,1,0:T(8,128)S(1)}, u32[]{:S(2)}, u32[]{:S(2)}) collective-permute-start(f32[25,8,128]{2,1,0:T(8,128)} %get-tuple-element.53), channel_id=1, source_target_pairs={{0,28},{4,0},{8,4},{12,8},{16,12},{20,16},{24,20},{28,24},{1,29},{... | collective-permute-start | bytes 307208 | tf_op jit(solution)/shard_map/ppermute | solution.py:807
  75.4 0.8 slice.130
  76.2 0.8 slice.125
  77.1 0.6 collective-permute-done.14.refs_1_
  77.6 0.9 slice_add_fusion.5
  78.5 2.9 %collective-permute-start.17 = (f32[25,8,128]{2,1,0:T(8,128)S(1)}, f32[25,8,128]{2,1,0:T(8,128)S(1)}, u32[]{:S(2)}, u32[]{:S(2)}) collective-permute-start(f32[25,8,128]{2,1,0:T(8,128)S(1)} %pad_maximum_fusion.5), channel_id=1, source_target_pairs={{0,3},{1,0},{2,1},{3,2},{4,7},{5,4},{6,5},{7,6},{8,11},{9,8},{10,9... | collective-permute-start | bytes 307208 | tf_op jit(solution)/shard_map/ppermute | solution.py:807
  81.4 1.0 collective-permute-start.16
  82.4 9.5 %interface1.1 = (f32[125,8,128]{2,1,0:T(8,128)}, f32[125,8,128]{2,1,0:T(8,128)}, f32[125,8,128]{2,1,0:T(8,128)}, f32[6,128,128]{2,1,0:T(8,128)}, f32[8,128]{1,0:T(8,128)}, /*index=5*/f32[160,128]{1,0:T(8,128)}) custom-call(f32[256,128]{1,0:T(8,128)} %copy-done, f32[256,128]{1,0:T(8,128)} %copy-done.5, f32[256,128]{1,0:T(8,128)} %copy-done.6, ...), custom_call_target="tpu_custom_call" | custom-call | flops 40000000 | bytes 8000000 | tf_op jit(solution)/shard_map/interface1/pallas_call | solution.py:901
  91.9 1.3 %slice.133.refs_5_ = f32[40,128]{1,0:T(8,128)} slice(f32[160,128]{1,0:T(8,128)} %get-tuple-element.60.refs_12_), slice={[0:40], [0:128]} | slice | bytes 40960 | tf_op jit(solution)/shard_map/slice | solution.py:878
  93.2 10.2 %interface2.1 = (f32[8,128]{1,0:T(8,128)}, f32[160,128]{1,0:T(8,128)}, f32[8,3,3,128]{3,2,1,0:T(4,128)}) custom-call(f32[40,128,128]{2,1,0:T(8,128)} %constant.50.clone.refs_8_.refs_0_, f32[128,256]{1,0:T(8,128)} %pad.8.refs_9_.refs_1_, f32[160,8]{1,0:T(8,128)} %constant_dynamic-slice_fusion.1.refs_10_.refs_2_, f32[8,128]{1,0:T(8,128)} %pad.9.refs_11_.refs_3_, ...), custom_call_target="tpu_custom_call" | custom-call | flops 40000000 | bytes 8000000 | tf_op jit(solution)/shard_map/interface2/pallas_call | solution.py:912
  103.4 0.9 copy.32
  104.2 1.3 %slice.144.refs_5_ = f32[40,128]{1,0:T(8,128)} slice(f32[160,128]{1,0:T(8,128)} %get-tuple-element.74), slice={[0:40], [0:128]} | slice | bytes 40960 | tf_op jit(solution)/shard_map/slice | solution.py:878
  105.6 0.6 copy-done.14
  106.2 4.1 %advance.4 = (f32[125,8,128]{2,1,0:T(8,128)}, f32[125,8,128]{2,1,0:T(8,128)}, f32[125,8,128]{2,1,0:T(8,128)}, f32[25,8,128]{2,1,0:T(8,128)}, f32[25,8,128]{2,1,0...) custom-call(f32[125,8,128]{2,1,0:T(8,128)} %get-tuple-element.51.refs_0_, f32[25,8,128]{2,1,0:T(8,128)} %copy-done.8, ...), custom_call_target="tpu_custom_call" | custom-call | flops 20000000 | bytes 4000000 | tf_op jit(solution)/shard_map/advance/pallas_call | solution.py:887
  110.4 4.1 %collective-permute-start.19 = (f32[25,8,128]{2,1,0:T(8,128)}, f32[25,8,128]{2,1,0:T(8,128)S(1)}, u32[]{:S(2)}, u32[]{:S(2)}) collective-permute-start(f32[25,8,128]{2,1,0:T(8,128)} %get-tuple-element.66), channel_id=1, source_target_pairs={{0,28},{4,0},{8,4},{12,8},{16,12},{20,16},{24,20},{28,24},{1,29},{... | collective-permute-start | bytes 307208 | tf_op jit(solution)/shard_map/ppermute | solution.py:807
  114.5 0.9 pad_maximum_fusion
  115.4 0.8 slice.141
  116.3 0.8 slice.136
  117.1 0.8 collective-permute-done.18.refs_1_
  117.9 0.9 slice_add_fusion.1
  118.8 0.7 collective-permute-start.21
  119.5 1.1 collective-permute-start.20
  120.6 0.7 slice_reduce_fusion
  121.3 2.7 %collective-permute-done.21.refs_4_ = f32[25,8,128]{2,1,0:T(8,128)S(1)} collective-permute-done((f32[25,8,128]{2,1,0:T(8,128)S(1)}, f32[25,8,128]{2,1,0:T(8,128)S(1)}, u32[]{:S(2)}, u32[]{:S(2)}) %collective-permute-start.21) | collective-permute-done | bytes 102432 | tf_op jit(solution)/shard_map/ppermute | solution.py:807
  124.0 0.6 copy-done.16
  124.7 2.8 %advance.5 = (f32[3,125,2,128]{3,2,1,0:T(2,128)}, f32[3,125,2,128]{3,2,1,0:T(2,128)}) custom-call(f32[125,8,128]{2,1,0:T(8,128)} %get-tuple-element.64.refs_0_, f32[25,8,128]{2,1,0:T(8,128)} %copy-done.10, f32[25,8,128]{2,1,0:T(8,128)} %copy-done.11, f32[25,8,128]{2,1,0:T(8,128)} %copy-done.17, f32[25,8,128]{2,1,0:T(8,128)} %copy-done.16, ...), custom_call_target="tpu_custom_call" | custom-call | flops 20000000 | bytes 4000000 | tf_op jit(solution)/shard_map/advance/pallas_call | solution.py:887
  (85 shorter events, 0.4 us)
Async XLA Ops:
  3.0 22.1 %copy-start.22 = (s32[256]{0:T(256)S(1)}, s32[256]{0:T(256)}, u32[]{:S(2)}) copy-start(s32[256]{0:T(256)} %refs_13_.1) | copy-start | bytes 3076
  3.0 22.4 %copy-start.21 = (f32[80,256]{1,0:T(8,128)S(1)}, f32[80,256]{1,0:T(8,128)}, u32[]{:S(2)}) copy-start(f32[80,256]{1,0:T(8,128)} %constant.47.clone) | copy-start | bytes 245764
  3.0 23.4 %copy-start.20 = (f32[320,8]{1,0:T(8,128)S(1)}, f32[320,8]{1,0:T(8,128)}, u32[]{:S(2)}) copy-start(f32[320,8]{1,0:T(8,128)} %constant.49.clone) | copy-start | bytes 30724
  3.0 24.0 %copy-start.24 = (f32[8,80]{1,0:T(8,128)S(1)}, f32[8,80]{1,0:T(8,128)}, u32[]{:S(2)}) copy-start(f32[8,80]{1,0:T(8,128)} %constant.48.clone) | copy-start | bytes 7684
  5.0 47.7 %copy-start.25 = (f32[3]{0:T(128)S(1)}, f32[3]{0:T(128)}, u32[]{:S(2)}) copy-start(f32[3]{0:T(128)} %param.25) | copy-start | bytes 40
  5.0 47.7 %copy-start.26 = (f32[3]{0:T(128)S(1)}, f32[3]{0:T(128)}, u32[]{:S(2)}) copy-start(f32[3]{0:T(128)} %param.24) | copy-start | bytes 40
  13.1 18.5 %collective-permute-start.4 = (f32[64,128]{1,0:T(8,128)}, f32[64,128]{1,0:T(8,128)S(1)}, u32[]{:S(2)}, u32[]{:S(2)}) collective-permute-start(f32[64,128]{1,0:T(8,128)} %gather.1), channel_id=1, source_target_pairs={{0,3},{1,0},{2,1},{3,2},{4,7},{5,4},{6,5},{7,6},{8,11},{9,8},{10,9... | collective-permute-start | bytes 98312 | tf_op jit(solution)/shard_map/ppermute | solution.py:807
  13.1 18.5 %collective-permute-start.5 = (f32[64,128]{1,0:T(8,128)}, f32[64,128]{1,0:T(8,128)S(1)}, u32[]{:S(2)}, u32[]{:S(2)}) collective-permute-start(f32[64,128]{1,0:T(8,128)} %gather.1), channel_id=1, source_target_pairs={{0,2},{1,3},{2,0},{3,1},{4,6},{5,7},{6,4},{7,5},{8,10},{9,11},{10,... | collective-permute-start | bytes 98312 | tf_op jit(solution)/shard_map/ppermute | solution.py:807
  15.8 15.8 %collective-permute-start.6 = (f32[64,128]{1,0:T(8,128)}, f32[64,128]{1,0:T(8,128)S(1)}, u32[]{:S(2)}, u32[]{:S(2)}) collective-permute-start(f32[64,128]{1,0:T(8,128)} %gather.1), channel_id=1, source_target_pairs={{0,1},{1,2},{2,3},{3,0},{4,5},{5,6},{6,7},{7,4},{8,9},{9,10},{10,1... | collective-permute-start | bytes 98312 | tf_op jit(solution)/shard_map/ppermute | solution.py:807
  20.8 13.3 %collective-permute-start = (f32[25,8,128]{2,1,0:T(8,128)}, f32[25,8,128]{2,1,0:T(8,128)S(1)}, u32[]{:S(2)}, u32[]{:S(2)}) collective-permute-start(f32[25,8,128]{2,1,0:T(8,128)} %get-tuple-element.44), channel_id=1, source_target_pairs={{0,4},{4,8},{8,12},{12,16},{16,20},{20,24},{24,28},{28,0},{1,5},{5... | collective-permute-start | bytes 307208 | tf_op jit(solution)/shard_map/ppermute | solution.py:807
  22.0 14.0 %collective-permute-start.1 = (f32[25,8,128]{2,1,0:T(8,128)}, f32[25,8,128]{2,1,0:T(8,128)S(1)}, u32[]{:S(2)}, u32[]{:S(2)}) collective-permute-start(f32[25,8,128]{2,1,0:T(8,128)} %get-tuple-element.45), channel_id=1, source_target_pairs={{0,28},{4,0},{8,4},{12,8},{16,12},{20,16},{24,20},{28,24},{1,29},{... | collective-permute-start | bytes 307208 | tf_op jit(solution)/shard_map/ppermute | solution.py:807
  32.4 24.3 %copy-start = (f32[256,128]{1,0:T(8,128)}, f32[256,128]{1,0:T(8,128)S(1)}, u32[]{:S(2)}) copy-start(f32[256,128]{1,0:T(8,128)S(1)} %pad_maximum_fusion.1.refs_0_) | copy-start | bytes 393220
  32.4 14.1 %collective-permute-start.10 = (f32[256,128]{1,0:T(8,128)S(1)}, f32[256,128]{1,0:T(8,128)S(1)}, u32[]{:S(2)}, u32[]{:S(2)}) collective-permute-start(f32[256,128]{1,0:T(8,128)S(1)} %pad_maximum_fusion.1.refs_0_), channel_id=1, source_target_pairs={{0,16},{4,20},{8,24},{12,28},{16,0},{20,4},{24,8},{28,12},{1,17},{... | collective-permute-start | bytes 393224 | tf_op jit(solution)/shard_map/ppermute | solution.py:807
  32.8 18.0 %collective-permute-start.11 = (f32[256,128]{1,0:T(8,128)S(1)}, f32[256,128]{1,0:T(8,128)S(1)}, u32[]{:S(2)}, u32[]{:S(2)}) collective-permute-start(f32[256,128]{1,0:T(8,128)S(1)} %pad_maximum_fusion.1.refs_0_), channel_id=1, source_target_pairs={{0,12},{4,16},{8,20},{12,24},{16,28},{20,0},{24,4},{28,8},{1,13},{... | collective-permute-start | bytes 393224 | tf_op jit(solution)/shard_map/ppermute | solution.py:807
  34.1 16.7 %collective-permute-start.12 = (f32[256,128]{1,0:T(8,128)S(1)}, f32[256,128]{1,0:T(8,128)S(1)}, u32[]{:S(2)}, u32[]{:S(2)}) collective-permute-start(f32[256,128]{1,0:T(8,128)S(1)} %pad_maximum_fusion.1.refs_0_), channel_id=1, source_target_pairs={{0,8},{4,12},{8,16},{12,20},{16,24},{20,28},{24,0},{28,4},{1,9},{5... | collective-permute-start | bytes 393224 | tf_op jit(solution)/shard_map/ppermute | solution.py:807
  34.2 31.6 %copy-start.12 = (f32[25,8,128]{2,1,0:T(8,128)}, f32[25,8,128]{2,1,0:T(8,128)S(1)}, u32[]{:S(2)}) copy-start(f32[25,8,128]{2,1,0:T(8,128)S(1)} %collective-permute-done.refs_1_) | copy-start | bytes 307204
  34.2 17.5 %collective-permute-start.13 = (f32[256,128]{1,0:T(8,128)S(1)}, f32[256,128]{1,0:T(8,128)S(1)}, u32[]{:S(2)}, u32[]{:S(2)}) collective-permute-start(f32[256,128]{1,0:T(8,128)S(1)} %pad_maximum_fusion.1.refs_0_), channel_id=1, source_target_pairs={{0,4},{4,8},{8,12},{12,16},{16,20},{20,24},{24,28},{28,0},{1,5},{5... | collective-permute-start | bytes 393224 | tf_op jit(solution)/shard_map/ppermute | solution.py:807
  36.1 29.7 %copy-start.13 = (f32[25,8,128]{2,1,0:T(8,128)}, f32[25,8,128]{2,1,0:T(8,128)S(1)}, u32[]{:S(2)}) copy-start(f32[25,8,128]{2,1,0:T(8,128)S(1)} %collective-permute-done.1.refs_2_) | copy-start | bytes 307204
  36.1 16.7 %collective-permute-start.7 = (f32[256,128]{1,0:T(8,128)S(1)}, f32[256,128]{1,0:T(8,128)S(1)}, u32[]{:S(2)}, u32[]{:S(2)}) collective-permute-start(f32[256,128]{1,0:T(8,128)S(1)} %pad_maximum_fusion.1.refs_0_), channel_id=1, source_target_pairs={{0,28},{4,0},{8,4},{12,8},{16,12},{20,16},{24,20},{28,24},{1,29},{... | collective-permute-start | bytes 393224 | tf_op jit(solution)/shard_map/ppermute | solution.py:807
  46.5 10.2 %copy-start.1 = (f32[256,128]{1,0:T(8,128)}, f32[256,128]{1,0:T(8,128)S(1)}, u32[]{:S(2)}) copy-start(f32[256,128]{1,0:T(8,128)S(1)} %collective-permute-done.10.refs_4_) | copy-start | bytes 393220
  46.5 6.3 %collective-permute-start.8 = (f32[256,128]{1,0:T(8,128)S(1)}, f32[256,128]{1,0:T(8,128)S(1)}, u32[]{:S(2)}, u32[]{:S(2)}) collective-permute-start(f32[256,128]{1,0:T(8,128)S(1)} %pad_maximum_fusion.1.refs_0_), channel_id=1, source_target_pairs={{0,24},{4,28},{8,0},{12,4},{16,8},{20,12},{24,16},{28,20},{1,25},{... | collective-permute-start | bytes 393224 | tf_op jit(solution)/shard_map/ppermute | solution.py:807
  50.8 5.9 %copy-start.2 = (f32[256,128]{1,0:T(8,128)}, f32[256,128]{1,0:T(8,128)S(1)}, u32[]{:S(2)}) copy-start(f32[256,128]{1,0:T(8,128)S(1)} %collective-permute-done.11.refs_5_) | copy-start | bytes 393220
  50.8 5.2 %collective-permute-start.9 = (f32[256,128]{1,0:T(8,128)S(1)}, f32[256,128]{1,0:T(8,128)S(1)}, u32[]{:S(2)}, u32[]{:S(2)}) collective-permute-start(f32[256,128]{1,0:T(8,128)S(1)} %pad_maximum_fusion.1.refs_0_), channel_id=1, source_target_pairs={{0,20},{4,24},{8,28},{12,0},{16,4},{20,8},{24,12},{28,16},{1,21},{... | collective-permute-start | bytes 393224 | tf_op jit(solution)/shard_map/ppermute | solution.py:807
  50.9 5.8 %copy-start.3 = (f32[256,128]{1,0:T(8,128)}, f32[256,128]{1,0:T(8,128)S(1)}, u32[]{:S(2)}) copy-start(f32[256,128]{1,0:T(8,128)S(1)} %collective-permute-done.12.refs_6_) | copy-start | bytes 393220
  50.9 14.9 %collective-permute-start.3 = (f32[25,8,128]{2,1,0:T(8,128)S(1)}, f32[25,8,128]{2,1,0:T(8,128)S(1)}, u32[]{:S(2)}, u32[]{:S(2)}) collective-permute-start(f32[25,8,128]{2,1,0:T(8,128)S(1)} %pad_maximum_fusion.3), channel_id=1, source_target_pairs={{0,3},{1,0},{2,1},{3,2},{4,7},{5,4},{6,5},{7,6},{8,11},{9,8},{10,9... | collective-permute-start | bytes 307208 | tf_op jit(solution)/shard_map/ppermute | solution.py:807
  51.7 5.0 %copy-start.4 = (f32[256,128]{1,0:T(8,128)}, f32[256,128]{1,0:T(8,128)S(1)}, u32[]{:S(2)}) copy-start(f32[256,128]{1,0:T(8,128)S(1)} %collective-permute-done.13.refs_7_) | copy-start | bytes 393220
  51.7 14.1 %collective-permute-start.2 = (f32[25,8,128]{2,1,0:T(8,128)S(1)}, f32[25,8,128]{2,1,0:T(8,128)S(1)}, u32[]{:S(2)}, u32[]{:S(2)}) collective-permute-start(f32[25,8,128]{2,1,0:T(8,128)S(1)} %pad_maximum_fusion.2), channel_id=1, source_target_pairs={{0,1},{1,2},{2,3},{3,0},{4,5},{5,6},{6,7},{7,4},{8,9},{9,10},{10,1... | collective-permute-start | bytes 307208 | tf_op jit(solution)/shard_map/ppermute | solution.py:807
  52.8 4.0 %copy-start.5 = (f32[256,128]{1,0:T(8,128)}, f32[256,128]{1,0:T(8,128)S(1)}, u32[]{:S(2)}) copy-start(f32[256,128]{1,0:T(8,128)S(1)} %collective-permute-done.7.refs_1_) | copy-start | bytes 393220
  52.8 4.0 %copy-start.6 = (f32[256,128]{1,0:T(8,128)}, f32[256,128]{1,0:T(8,128)S(1)}, u32[]{:S(2)}) copy-start(f32[256,128]{1,0:T(8,128)S(1)} %collective-permute-done.8.refs_2_) | copy-start | bytes 393220
  56.0 0.7 copy-start.7
  65.8 0.6 copy-start.18
  65.8 0.7 copy-start.19
  70.6 7.0 %collective-permute-start.14 = (f32[25,8,128]{2,1,0:T(8,128)}, f32[25,8,128]{2,1,0:T(8,128)S(1)}, u32[]{:S(2)}, u32[]{:S(2)}) collective-permute-start(f32[25,8,128]{2,1,0:T(8,128)} %get-tuple-element.52), channel_id=1, source_target_pairs={{0,4},{4,8},{8,12},{12,16},{16,20},{20,24},{24,28},{28,0},{1,5},{5... | collective-permute-start | bytes 307208 | tf_op jit(solution)/shard_map/ppermute | solution.py:807
  72.7 5.0 %collective-permute-start.15 = (f32[25,8,128]{2,1,0:T(8,128)}, f32[25,8,128]{2,1,0:T(8,128)S(1)}, u32[]{:S(2)}, u32[]{:S(2)}) collective-permute-start(f32[25,8,128]{2,1,0:T(8,128)} %get-tuple-element.53), channel_id=1, source_target_pairs={{0,28},{4,0},{8,4},{12,8},{16,12},{20,16},{24,20},{28,24},{1,29},{... | collective-permute-start | bytes 307208 | tf_op jit(solution)/shard_map/ppermute | solution.py:807
  77.6 14.2 %copy-start.8 = (f32[25,8,128]{2,1,0:T(8,128)}, f32[25,8,128]{2,1,0:T(8,128)S(1)}, u32[]{:S(2)}) copy-start(f32[25,8,128]{2,1,0:T(8,128)S(1)} %collective-permute-done.14.refs_1_) | copy-start | bytes 307204
  77.6 14.2 %copy-start.9 = (f32[25,8,128]{2,1,0:T(8,128)}, f32[25,8,128]{2,1,0:T(8,128)S(1)}, u32[]{:S(2)}) copy-start(f32[25,8,128]{2,1,0:T(8,128)S(1)} %collective-permute-done.15.refs_2_) | copy-start | bytes 307204
  78.5 27.0 %collective-permute-start.17 = (f32[25,8,128]{2,1,0:T(8,128)S(1)}, f32[25,8,128]{2,1,0:T(8,128)S(1)}, u32[]{:S(2)}, u32[]{:S(2)}) collective-permute-start(f32[25,8,128]{2,1,0:T(8,128)S(1)} %pad_maximum_fusion.5), channel_id=1, source_target_pairs={{0,3},{1,0},{2,1},{3,2},{4,7},{5,4},{6,5},{7,6},{8,11},{9,8},{10,9... | collective-permute-start | bytes 307208 | tf_op jit(solution)/shard_map/ppermute | solution.py:807
  81.4 24.2 %collective-permute-start.16 = (f32[25,8,128]{2,1,0:T(8,128)S(1)}, f32[25,8,128]{2,1,0:T(8,128)S(1)}, u32[]{:S(2)}, u32[]{:S(2)}) collective-permute-start(f32[25,8,128]{2,1,0:T(8,128)S(1)} %pad_maximum_fusion.4), channel_id=1, source_target_pairs={{0,1},{1,2},{2,3},{3,0},{4,5},{5,6},{6,7},{7,4},{8,9},{9,10},{10,1... | collective-permute-start | bytes 307208 | tf_op jit(solution)/shard_map/ppermute | solution.py:807
  103.4 11.1 %slice-start = ((f32[8,63,3,128]{3,0,2,1:T(8,128)}), f32[8,60,3,128]{3,0,2,1:T(8,128)S(1)}, s32[]{:S(2)}) async-start(f32[8,63,3,128]{3,0,2,1:T(8,128)} %param.21), calls=%async_computation | async-start | bytes 1474560 | tf_op jit(solution)/shard_map/slice | solution.py:922
  103.4 17.3 %copy-start.23 = (f32[8,128]{1,0:T(8,128)S(1)}, f32[8,128]{1,0:T(8,128)}, u32[]{:S(2)}) copy-start(f32[8,128]{1,0:T(8,128)} %get-tuple-element.80) | copy-start | bytes 12292
  105.6 0.6 copy-start.14
  105.6 0.7 copy-start.15
  110.3 7.5 %collective-permute-start.18 = (f32[25,8,128]{2,1,0:T(8,128)}, f32[25,8,128]{2,1,0:T(8,128)S(1)}, u32[]{:S(2)}, u32[]{:S(2)}) collective-permute-start(f32[25,8,128]{2,1,0:T(8,128)} %get-tuple-element.65), channel_id=1, source_target_pairs={{0,4},{4,8},{8,12},{12,16},{16,20},{20,24},{24,28},{28,0},{1,5},{5... | collective-permute-start | bytes 307208 | tf_op jit(solution)/shard_map/ppermute | solution.py:807
  110.4 7.5 %collective-permute-start.19 = (f32[25,8,128]{2,1,0:T(8,128)}, f32[25,8,128]{2,1,0:T(8,128)S(1)}, u32[]{:S(2)}, u32[]{:S(2)}) collective-permute-start(f32[25,8,128]{2,1,0:T(8,128)} %get-tuple-element.66), channel_id=1, source_target_pairs={{0,28},{4,0},{8,4},{12,8},{16,12},{20,16},{24,20},{28,24},{1,29},{... | collective-permute-start | bytes 307208 | tf_op jit(solution)/shard_map/ppermute | solution.py:807
  117.9 6.2 %copy-start.10 = (f32[25,8,128]{2,1,0:T(8,128)}, f32[25,8,128]{2,1,0:T(8,128)S(1)}, u32[]{:S(2)}) copy-start(f32[25,8,128]{2,1,0:T(8,128)S(1)} %collective-permute-done.18.refs_1_) | copy-start | bytes 307204
  117.9 6.2 %copy-start.11 = (f32[25,8,128]{2,1,0:T(8,128)}, f32[25,8,128]{2,1,0:T(8,128)S(1)}, u32[]{:S(2)}) copy-start(f32[25,8,128]{2,1,0:T(8,128)S(1)} %collective-permute-done.19.refs_2_) | copy-start | bytes 307204
  118.8 5.2 %collective-permute-start.21 = (f32[25,8,128]{2,1,0:T(8,128)S(1)}, f32[25,8,128]{2,1,0:T(8,128)S(1)}, u32[]{:S(2)}, u32[]{:S(2)}) collective-permute-start(f32[25,8,128]{2,1,0:T(8,128)S(1)} %pad_maximum_fusion.7), channel_id=1, source_target_pairs={{0,3},{1,0},{2,1},{3,2},{4,7},{5,4},{6,5},{7,6},{8,11},{9,8},{10,9... | collective-permute-start | bytes 307208 | tf_op jit(solution)/shard_map/ppermute | solution.py:807
  119.5 4.5 %collective-permute-start.20 = (f32[25,8,128]{2,1,0:T(8,128)S(1)}, f32[25,8,128]{2,1,0:T(8,128)S(1)}, u32[]{:S(2)}, u32[]{:S(2)}) collective-permute-start(f32[25,8,128]{2,1,0:T(8,128)S(1)} %pad_maximum_fusion.6), channel_id=1, source_target_pairs={{0,1},{1,2},{2,3},{3,0},{4,5},{5,6},{6,7},{7,4},{8,9},{9,10},{10,1... | collective-permute-start | bytes 307208 | tf_op jit(solution)/shard_map/ppermute | solution.py:807
  124.0 0.6 copy-start.16
  124.0 0.7 copy-start.17
